TPU v7x, 16 devices: a whole 2x2x2 slice. The times are simulated.
16 devices in a mesh: ty: 4 (over z, y), tx: 4 (over x, core).
Axes of the slice: x: 2, y: 2, z: 2, core: 2. Of those that a mesh axis runs over, the one named last changes fastest.
Arguments:
- x_tok: bfloat16 [4096, 2048], P('ty', 'tx')
- dy_tok: bfloat16 [4096, 2048], P('ty', 'tx')
- ln_gain: float32 [2048], P('tx')
- w_gate: bfloat16 [2048, 8192], P('tx', 'ty')
- w_up: bfloat16 [2048, 8192], P('tx', 'ty')
- w_down: bfloat16 [8192, 2048], P('ty', 'tx')
Outputs:
- output 1: bfloat16 [4096, 2048], P('ty', 'tx')
- output 2: bfloat16 [4096, 2048], P('ty', 'tx')
- output 3: float32 [2048, 8192], P('tx', 'ty')
- output 4: float32 [2048, 8192], P('tx', 'ty')
- output 5: float32 [8192, 2048], P('ty', 'tx')
- output 6: float32 [2048], P('tx')
All inputs are finite; a program needn't handle non-finite values.
Results may differ from a plain program's by a relative error of at most 0.00118.
Values are sent between devices in bfloat16 or wider.
A program may use at most 1 GiB of HBM per device.

v0:
```python
import jax
import jax.numpy as jnp
from jax import lax
from jax.sharding import PartitionSpec as P

LN_EPS = 1e-6


def contract_rows(left_op, right_op):
    return lax.dot_general(left_op, right_op, (((0,), (0,)), ((), ())), preferred_element_type=jnp.float32)


def contract_cols(left_op, right_op):
    return lax.dot_general(left_op, right_op, (((1,), (1,)), ((), ())), preferred_element_type=jnp.float32)


def solution(mesh):
    tx_size = mesh.shape["tx"]

    def local_step(x_blk, dy_blk, gain_blk, w_gate_blk, w_up_blk, w_down_blk):
        d_model = x_blk.shape[1] * tx_size
        x_float = x_blk.astype(jnp.float32)
        ln_stats = lax.psum(jnp.stack([jnp.sum(x_float, axis=1), jnp.sum(x_float * x_float, axis=1)]), "tx") / d_model
        mean_x = ln_stats[0][:, None]
        inv_std = lax.rsqrt(ln_stats[1][:, None] - mean_x * mean_x + LN_EPS)
        x_hat = (x_float - mean_x) * inv_std
        h_blk = (gain_blk * x_hat).astype(jnp.bfloat16)
        h_all = lax.all_gather(h_blk, "ty", axis=0, tiled=True)
        gate_pre = lax.psum_scatter(jnp.dot(h_all, w_gate_blk, preferred_element_type=jnp.float32),
                                    "tx", scatter_dimension=0, tiled=True)
        up_pre = lax.psum_scatter(jnp.dot(h_all, w_up_blk, preferred_element_type=jnp.float32),
                                  "tx", scatter_dimension=0, tiled=True)
        gate_sig = jax.nn.sigmoid(gate_pre)
        gate_swish = gate_pre * gate_sig
        act_blk = (gate_swish * up_pre).astype(jnp.bfloat16)
        act_all = lax.all_gather(act_blk, "tx", axis=0, tiled=True)
        mlp_out = lax.psum_scatter(jnp.dot(act_all, w_down_blk, preferred_element_type=jnp.float32),
                                   "ty", scatter_dimension=0, tiled=True)
        y_blk = (x_float + mlp_out).astype(jnp.bfloat16)

        dy_all = lax.all_gather(dy_blk, "ty", axis=0, tiled=True)
        dw_down_blk = contract_rows(act_all, dy_all)
        d_act = lax.psum_scatter(contract_cols(dy_all, w_down_blk), "tx", scatter_dimension=0, tiled=True)
        d_gate = (d_act * up_pre * gate_sig * (1.0 + gate_pre * (1.0 - gate_sig))).astype(jnp.bfloat16)
        d_up = (d_act * gate_swish).astype(jnp.bfloat16)
        d_gate_all = lax.all_gather(d_gate, "tx", axis=0, tiled=True)
        d_up_all = lax.all_gather(d_up, "tx", axis=0, tiled=True)
        dw_gate_blk = contract_rows(h_all, d_gate_all)
        dw_up_blk = contract_rows(h_all, d_up_all)
        d_hnorm = lax.psum_scatter(contract_cols(d_gate_all, w_gate_blk) + contract_cols(d_up_all, w_up_blk),
                                   "ty", scatter_dimension=0, tiled=True)
        value_a6 = d_hnorm * gain_blk
        bwd_stats = lax.psum(jnp.stack([jnp.sum(value_a6, axis=1), jnp.sum(value_a6 * x_hat, axis=1)]), "tx") / d_model
        dx_ln = inv_std * (value_a6 - bwd_stats[0][:, None] - x_hat * bwd_stats[1][:, None])
        dx_blk = (dy_blk.astype(jnp.float32) + dx_ln).astype(jnp.bfloat16)
        d_gain_blk = lax.psum(jnp.sum(d_hnorm * x_hat, axis=0), "ty")
        return (y_blk, dx_blk, dw_gate_blk, dw_up_blk, dw_down_blk, d_gain_blk)

    return jax.shard_map(
        local_step, mesh=mesh,
        in_specs=(P("ty", "tx"), P("ty", "tx"), P("tx"), P("tx", "ty"), P("tx", "ty"), P("ty", "tx")),
        out_specs=(P("ty", "tx"), P("ty", "tx"), P("tx", "ty"), P("tx", "ty"), P("ty", "tx"), P("tx")),
        check_vma=False)
```

profile of v0, /device:TPU:0, one launch (start us, length us, event | category | flops | bytes accessed | tf_op | source)
XLA Modules:
  0.0 1328.8 jit_solution(15651089622808205627)
XLA Ops:
  7.2 0.0 copy-start
  7.2 0.0 all-gather.6.cloned.1.call-start
  7.2 1.7 convert_reduce_fusion
  9.0 8.8 psum.21
  17.8 0.0 copy-start.3
  17.8 0.6 copy-done.3
  18.4 0.6 copy-done.5
  19.0 2.6 fusion.7
  21.6 0.0 all-gather.6.cloned.1.call-update
  21.6 0.0 all-gather.10.cloned.1.call-start
  21.7 0.7 all-gather.10.cloned.1.call-update
  22.4 0.0 reduce-scatter.8.cloned.1.call-start
  22.4 48.0 %all-gather.6.cloned.1.call-done = bf16[4096,512]{1,0:T(8,128)(2,1)} async-done(((bf16[1024,512]{1,0:T(8,128)(2,1)}), bf16[4096,512]{1,0:T(8,128)(2,1)}) %all-gather.6.cloned.1.call-update) | async-done | bytes 4194320 | tf_op jit(solution)/shard_map/all_gather | solution.py:28
  70.4 17.9 %fusion.18 = f32[4096,2048]{1,0:T(8,128)} fusion(bf16[4096,512]{1,0:T(8,128)(2,1)} %all-gather.6.cloned.1.call-done, bf16[512,2048]{1,0:T(8,128)(2,1)} %param.10), kind=kOutput, calls=%fused_computation.33 | convolution fusion | flops 8589934592 | bytes 39845888 | tf_op jit(solution)/shard_map/dot_general | solution.py:31
  88.3 0.0 reduce-scatter.8.cloned.1.call-update
  88.3 0.0 reduce-scatter.6.cloned.1.call-start
  88.4 0.0 copy-done
  88.4 17.6 %fusion.17 = f32[4096,2048]{1,0:T(8,128)} fusion(bf16[4096,512]{1,0:T(8,128)(2,1)} %all-gather.6.cloned.1.call-done, bf16[512,2048]{1,0:T(8,128)(2,1)S(1)} %copy-done), kind=kOutput, calls=%fused_computation.32 | convolution fusion | flops 8589934592 | bytes 39845888 | tf_op jit(solution)/shard_map/dot_general | solution.py:29
  106.0 0.0 reduce-scatter.6.cloned.1.call-update
  106.0 0.2 reduce-scatter.12.cloned.1.call-start
  106.2 14.5 %all-gather.10.cloned.1.call-done = bf16[4096,512]{1,0:T(8,128)(2,1)} async-done(((bf16[1024,512]{1,0:T(8,128)(2,1)}), bf16[4096,512]{1,0:T(8,128)(2,1)}) %all-gather.10.cloned.1.call-update) | async-done | bytes 4194320 | tf_op jit(solution)/shard_map/all_gather | solution.py:41
  120.7 18.0 %fusion.20 = f32[4096,2048]{1,0:T(8,128)} fusion(bf16[4096,512]{1,0:T(8,128)(2,1)} %all-gather.10.cloned.1.call-done, bf16[2048,512]{1,0:T(8,128)(2,1)} %param.11), kind=kOutput, calls=%fused_computation.35 | convolution fusion | flops 8589934592 | bytes 39845888 | tf_op jit(solution)/shard_map/dot_general | solution.py:14
  138.7 0.0 reduce-scatter.12.cloned.1.call-update
  138.7 0.0 all-gather.12.cloned.1.call-start
  138.7 212.4 %reduce-scatter.8.cloned.1.call-done = f32[1024,2048]{1,0:T(8,128)} async-done(((f32[4096,2048]{1,0:T(8,128)}), f32[1024,2048]{1,0:T(8,128)}) %reduce-scatter.8.cloned.1.call-update) | async-done | bytes 8388624 | tf_op jit(solution)/shard_map/reduce_scatter | solution.py:31
  351.1 230.3 %reduce-scatter.6.cloned.1.call-done = f32[1024,2048]{1,0:T(8,128)} async-done(((f32[4096,2048]{1,0:T(8,128)}), f32[1024,2048]{1,0:T(8,128)}) %reduce-scatter.6.cloned.1.call-update) | async-done | bytes 8388624 | tf_op jit(solution)/shard_map/reduce_scatter | solution.py:29
  581.4 230.3 %reduce-scatter.12.cloned.1.call-done = f32[1024,2048]{1,0:T(8,128)} async-done(((f32[4096,2048]{1,0:T(8,128)}), f32[1024,2048]{1,0:T(8,128)}) %reduce-scatter.12.cloned.1.call-update) | async-done | bytes 8388624 | tf_op jit(solution)/shard_map/reduce_scatter | solution.py:43
  811.7 15.3 %multiply_convert_fusion = (bf16[1024,2048]{1,0:T(8,128)(2,1)}, bf16[1024,2048]{1,0:T(8,128)(2,1)}, bf16[1024,2048]{1,0:T(8,128)(2,1)}) fusion(f32[1024,2048]{1,0:T(8,128)} %reduce-scatter.12.cloned.1.call-done, f32[1024,2048]{1,0:T(8,128)} %reduce-scatter.6.cloned.1.call-done, f32[1024,2048]{1,0:T(8,128)} %reduce-scatter.8.cloned.1.call-done), kind=kLoop, calls=%fused_computation | loop fusion | flops 31457280 | bytes 37748736 | tf_op jit(solution)/shard_map/convert_element_type | solution.py:45
  827.0 0.0 all-gather.12.cloned.1.call-update
  827.0 0.0 all-gather.14.cloned.1.call-start
  827.0 0.7 all-gather.14.cloned.1.call-update
  827.7 0.0 all-gather.8.cloned.1.call-start
  827.8 0.7 all-gather.8.cloned.1.call-update
  828.5 0.3 reduce-scatter.14.cloned.1.call-start
  828.7 103.5 %all-gather.12.cloned.1.call-done = bf16[4096,2048]{1,0:T(8,128)(2,1)} async-done(((bf16[1024,2048]{1,0:T(8,128)(2,1)}), bf16[4096,2048]{1,0:T(8,128)(2,1)}) %all-gather.12.cloned.1.call-update) | async-done | bytes 16777232 | tf_op jit(solution)/shard_map/all_gather | solution.py:46
  932.2 14.5 %fusion.21 = f32[4096,512]{1,0:T(8,128)} fusion(bf16[4096,2048]{1,0:T(8,128)(2,1)} %all-gather.12.cloned.1.call-done, bf16[512,2048]{1,0:T(8,128)(2,1)S(1)} %copy-done), kind=kOutput, calls=%fused_computation.36 | convolution fusion | flops 8589934592 | bytes 27262976 | tf_op jit(solution)/shard_map/dot_general | solution.py:14
  946.7 92.8 %all-gather.14.cloned.1.call-done = bf16[4096,2048]{1,0:T(8,128)(2,1)} async-done(((bf16[1024,2048]{1,0:T(8,128)(2,1)}), bf16[4096,2048]{1,0:T(8,128)(2,1)}) %all-gather.14.cloned.1.call-update) | async-done | bytes 16777232 | tf_op jit(solution)/shard_map/all_gather | solution.py:47
  1039.4 18.7 %convolution_add_fusion = f32[4096,512]{1,0:T(8,128)} fusion(f32[4096,512]{1,0:T(8,128)} %fusion.21, bf16[4096,2048]{1,0:T(8,128)(2,1)} %all-gather.14.cloned.1.call-done, bf16[512,2048]{1,0:T(8,128)(2,1)} %param.10), kind=kOutput, calls=%fused_computation.5 | convolution fusion | flops 8592031744 | bytes 35651584 | tf_op jit(solution)/shard_map/dot_general | solution.py:14
  1058.2 0.0 reduce-scatter.14.cloned.1.call-update
  1058.2 0.3 reduce-scatter.10.cloned.1.call-start
  1058.5 88.2 %all-gather.8.cloned.1.call-done = bf16[4096,2048]{1,0:T(8,128)(2,1)} async-done(((bf16[1024,2048]{1,0:T(8,128)(2,1)}), bf16[4096,2048]{1,0:T(8,128)(2,1)}) %all-gather.8.cloned.1.call-update) | async-done | bytes 16777232 | tf_op jit(solution)/shard_map/all_gather | solution.py:36
  1146.7 0.0 copy-done.10
  1146.7 14.4 %fusion.19 = f32[4096,512]{1,0:T(8,128)} fusion(bf16[4096,2048]{1,0:T(8,128)(2,1)} %all-gather.8.cloned.1.call-done, bf16[2048,512]{1,0:T(8,128)(2,1)S(1)} %copy-done.10), kind=kOutput, calls=%fused_computation.34 | convolution fusion | flops 8589934592 | bytes 27262976 | tf_op jit(solution)/shard_map/dot_general | solution.py:37
  1161.1 0.0 reduce-scatter.10.cloned.1.call-update
  1161.1 0.0 copy-start.8
  1161.1 0.0 slice-start
  1161.2 0.0 slice-start.1
  1161.2 17.1 %fusion.22 = f32[512,2048]{1,0:T(8,128)} fusion(bf16[4096,512]{1,0:T(8,128)(2,1)} %all-gather.6.cloned.1.call-done, bf16[4096,2048]{1,0:T(8,128)(2,1)} %all-gather.12.cloned.1.call-done), kind=kOutput, calls=%fused_computation.37 | convolution fusion | flops 8589934592 | bytes 25165824 | tf_op jit(solution)/shard_map/dot_general | solution.py:10
  1178.3 0.0 copy-done.8
  1178.3 0.0 copy-start.9
  1178.3 14.2 %fusion.23 = f32[512,2048]{1,0:T(8,128)} fusion(bf16[4096,512]{1,0:T(8,128)(2,1)S(1)} %copy-done.8, bf16[4096,2048]{1,0:T(8,128)(2,1)} %all-gather.14.cloned.1.call-done), kind=kOutput, calls=%fused_computation.38 | convolution fusion | flops 8589934592 | bytes 25165824 | tf_op jit(solution)/shard_map/dot_general | solution.py:10
  1192.5 0.0 slice-done
  1192.5 0.0 slice-done.2
  1192.6 0.0 copy-start.2
  1192.6 0.0 copy-start.6
  1192.6 0.0 copy-start.7
  1192.6 10.7 fusion.24
  1203.3 28.8 %reduce-scatter.14.cloned.1.call-done = f32[1024,512]{1,0:T(8,128)} async-done(((f32[4096,512]{1,0:T(8,128)}), f32[1024,512]{1,0:T(8,128)}) %reduce-scatter.14.cloned.1.call-update) | async-done | bytes 2097168 | tf_op jit(solution)/shard_map/reduce_scatter | solution.py:50
  1232.1 2.6 fusion.13
  1234.7 9.6 psum.23
  1244.3 6.2 psum.22
  1250.5 66.9 %reduce-scatter.10.cloned.1.call-done = f32[1024,512]{1,0:T(8,128)} async-done(((f32[4096,512]{1,0:T(8,128)}), f32[1024,512]{1,0:T(8,128)}) %reduce-scatter.10.cloned.1.call-update) | async-done | bytes 2097168 | tf_op jit(solution)/shard_map/reduce_scatter | solution.py:37
  1317.4 4.1 fusion.12
  1321.5 0.0 copy-done.1
  (21 shorter events, 0.1 us)
Async XLA Ops:
  7.2 81.2 %copy-start = (bf16[512,2048]{1,0:T(8,128)(2,1)S(1)}, bf16[512,2048]{1,0:T(8,128)(2,1)}, u32[]{:S(2)}) copy-start(bf16[512,2048]{1,0:T(8,128)(2,1)} %param.9) | copy-start | bytes 6291460
  7.2 63.2 %all-gather.6.cloned.1.call-start = ((), (), s32[]{:S(2)}) async-start(), calls=%async_computation.5 | async-start | bytes 5242880 | tf_op jit(solution)/shard_map/all_gather | solution.py:28
  17.8 0.6 copy-start.3
  18.4 0.6 copy-start.5
  21.6 99.1 %all-gather.10.cloned.1.call-start = ((), (), s32[]{:S(2)}) async-start(), calls=%async_computation.10 | async-start | bytes 5242880 | tf_op jit(solution)/shard_map/all_gather | solution.py:41
  22.4 328.7 %reduce-scatter.8.cloned.1.call-start = ((), (), s32[]{:S(2)}) async-start(), calls=%async_computation.7 | async-start | bytes 41943040 | tf_op jit(solution)/shard_map/reduce_scatter | solution.py:31
  88.3 493.1 %reduce-scatter.6.cloned.1.call-start = ((), (), s32[]{:S(2)}) async-start(), calls=%async_computation.6 | async-start | bytes 41943040 | tf_op jit(solution)/shard_map/reduce_scatter | solution.py:29
  106.0 705.7 %reduce-scatter.12.cloned.1.call-start = ((), (), s32[]{:S(2)}) async-start(), calls=%async_computation.11 | async-start | bytes 41943040 | tf_op jit(solution)/shard_map/reduce_scatter | solution.py:43
  138.7 793.5 %all-gather.12.cloned.1.call-start = ((), (), s32[]{:S(2)}) async-start(), calls=%async_computation.12 | async-start | bytes 20971520 | tf_op jit(solution)/shard_map/all_gather | solution.py:46
  827.0 212.5 %all-gather.14.cloned.1.call-start = ((), (), s32[]{:S(2)}) async-start(), calls=%async_computation.13 | async-start | bytes 20971520 | tf_op jit(solution)/shard_map/all_gather | solution.py:47
  827.7 319.0 %all-gather.8.cloned.1.call-start = ((), (), s32[]{:S(2)}) async-start(), calls=%async_computation.8 | async-start | bytes 20971520 | tf_op jit(solution)/shard_map/all_gather | solution.py:36
  828.5 403.6 %reduce-scatter.14.cloned.1.call-start = ((), (), s32[]{:S(2)}) async-start(), calls=%async_computation.14 | async-start | bytes 10485760 | tf_op jit(solution)/shard_map/reduce_scatter | solution.py:50
  1058.2 88.5 %copy-start.10 = (bf16[2048,512]{1,0:T(8,128)(2,1)S(1)}, bf16[2048,512]{1,0:T(8,128)(2,1)}, u32[]{:S(2)}) copy-start(bf16[2048,512]{1,0:T(8,128)(2,1)} %param.11) | copy-start | bytes 6291460
  1058.2 259.2 %reduce-scatter.10.cloned.1.call-start = ((), (), s32[]{:S(2)}) async-start(), calls=%async_computation.9 | async-start | bytes 10485760 | tf_op jit(solution)/shard_map/reduce_scatter | solution.py:37
  1161.1 17.1 %copy-start.8 = (bf16[4096,512]{1,0:T(8,128)(2,1)S(1)}, bf16[4096,512]{1,0:T(8,128)(2,1)}, u32[]{:S(2)}) copy-start(bf16[4096,512]{1,0:T(8,128)(2,1)} %all-gather.6.cloned.1.call-done) | copy-start | bytes 12582916
  1161.1 31.4 %slice-start = ((s8[16777216]{0:T(1024)(128)(4,1)}), s8[4194304]{0:T(1024)(128)(4,1)S(1)}, s32[]{:S(2)}) async-start(s8[16777216]{0:T(1024)(128)(4,1)} %bitcast.37), calls=%async_computation.15 | async-start | bytes 8388608
  1161.2 31.4 %slice-start.1 = ((s8[16777216]{0:T(1024)(128)(4,1)}), s8[4194304]{0:T(1024)(128)(4,1)S(1)}, s32[]{:S(2)}) async-start(s8[16777216]{0:T(1024)(128)(4,1)} %bitcast.37), calls=%async_computation.16 | async-start | bytes 8388608
  1178.3 14.2 %slice-start.2 = ((s8[16777216]{0:T(1024)(128)(4,1)}), s8[4194304]{0:T(1024)(128)(4,1)S(1)}, s32[]{:S(2)}) async-start(s8[16777216]{0:T(1024)(128)(4,1)} %bitcast.37), calls=%async_computation.17 | async-start | bytes 8388608
  1178.3 14.2 %slice-start.3 = ((s8[16777216]{0:T(1024)(128)(4,1)}), s8[4194304]{0:T(1024)(128)(4,1)S(1)}, s32[]{:S(2)}) async-start(s8[16777216]{0:T(1024)(128)(4,1)} %bitcast.37), calls=%async_computation.18 | async-start | bytes 8388608
  1178.3 14.2 %copy-start.9 = (bf16[4096,512]{1,0:T(8,128)(2,1)S(1)}, bf16[4096,512]{1,0:T(8,128)(2,1)}, u32[]{:S(2)}) copy-start(bf16[4096,512]{1,0:T(8,128)(2,1)} %all-gather.10.cloned.1.call-done) | copy-start | bytes 12582916
  1192.6 39.5 %copy-start.2 = (bf16[1024,512]{1,0:T(8,128)(2,1)S(1)}, bf16[1024,512]{1,0:T(8,128)(2,1)}, u32[]{:S(2)}) copy-start(bf16[1024,512]{1,0:T(8,128)(2,1)} %param.6) | copy-start | bytes 3145732
  1192.6 39.5 %copy-start.4 = (f32[1,1024]{1,0:T(1,128)S(1)}, f32[1,1024]{1,0:T(1,128)}, u32[]{:S(2)}) copy-start(f32[1,1024]{1,0:T(1,128)} %copy-done.3) | copy-start | bytes 12292
  1192.6 39.5 %copy-start.6 = (f32[1024]{0:T(1024)S(1)}, f32[1024]{0:T(1024)}, u32[]{:S(2)}) copy-start(f32[1024]{0:T(1024)} %copy-done.5) | copy-start | bytes 12292
  1192.6 39.5 %copy-start.7 = (f32[512]{0:T(512)S(1)}, f32[512]{0:T(512)}, u32[]{:S(2)}) copy-start(f32[512]{0:T(512)} %param.8) | copy-start | bytes 6148
  1317.4 4.1 copy-start.1
Sparse Core Ops, SparseCore 0:
  21.8 48.6 all-gather.5
  72.2 48.4 all-gather.9
  123.3 227.8 reduce-scatter.7
  353.5 227.8 reduce-scatter.5
  583.8 227.8 reduce-scatter.11
  827.1 105.0 all-gather.11
  934.3 105.0 all-gather.13
  1041.6 105.0 all-gather.7
  1149.7 82.3 reduce-scatter.13
  1235.0 82.4 reduce-scatter.9
where the time goes:
time: 1340 us; the launch traced here: 1330 us
  waiting for transfers between devices  1120 us (84%)
  matrix products  143 us (11%)
  other arithmetic  26.3 us (2%)
  blocking collectives  24.6 us (2%)
  between operations  14.9 us (1%)
    reduce_scatter x1, waiting for transfers between devices, local_step(): lax.psum_scatter(jnp.dot(h_all, w_gate_blk, preferred_element_type=jnp.fl...  230 us
    reduce_scatter x1, waiting for transfers between devices, local_step(): lax.psum_scatter(contract_cols(dy_all, w_down_blk), 'tx', scatter_dimensi...  230 us
    reduce_scatter x1, waiting for transfers between devices, local_step(): lax.psum_scatter(jnp.dot(h_all, w_up_blk, preferred_element_type=jnp.floa...  212 us
    all_gather x1, waiting for transfers between devices, local_step(): d_gate_all = lax.all_gather(d_gate, 'tx', axis=0, tiled=True)  103 us
    all_gather x1, waiting for transfers between devices, local_step(): d_up_all = lax.all_gather(d_up, 'tx', axis=0, tiled=True)  92.8 us
    all_gather x1, waiting for transfers between devices, local_step(): act_all = lax.all_gather(act_blk, 'tx', axis=0, tiled=True)  88.2 us
    reduce_scatter x1, waiting for transfers between devices, local_step(): lax.psum_scatter(jnp.dot(act_all, w_down_blk, preferred_element_type=jnp....  66.9 us
    dot_general x3, matrix products, contract_cols(): lax.dot_general(left_op, right_op, (((1,), (1,)), ((), ())), preferred_el...  51.2 us
  transfers between devices with their start and end apart: 10, of which 10 were waited for; matrix products, arithmetic and copies ran while one was open for 11% of the time, Pallas kernels for 0%

commit v1 on v0

v1 whole, which is shorter than its diff:
```python
import jax
import jax.numpy as jnp
from jax import lax
from jax.sharding import PartitionSpec as P

LN_EPS = 1e-6
CHIP = [[0, 1], [2, 3]]


def contract_rows(left_op, right_op):
    return lax.dot_general(left_op, right_op, (((0,), (0,)), ((), ())), preferred_element_type=jnp.float32)


def contract_cols(left_op, right_op):
    return lax.dot_general(left_op, right_op, (((1,), (1,)), ((), ())), preferred_element_type=jnp.float32)


def solution(mesh):
    tx_size = mesh.shape["tx"]

    def local_step(x_blk, dy_blk, gain_blk, w_gate_blk, w_up_blk, w_down_blk):
        rows, cols = x_blk.shape
        d_model = cols * tx_size
        f_loc = w_gate_blk.shape[1]
        half = f_loc // 2
        core = lax.rem(lax.axis_index("tx"), 2)
        tx = lax.axis_index("tx")

        def pick(w):
            return lax.dynamic_slice_in_dim(w, core * half, half, axis=1)

        w_gate_all = pick(lax.all_gather(w_gate_blk, "tx", axis=0, tiled=True))
        w_up_all = pick(lax.all_gather(w_up_blk, "tx", axis=0, tiled=True))
        w_down_all = lax.dynamic_slice_in_dim(lax.all_gather(w_down_blk, "tx", axis=1, tiled=True), core * half, half, 0)
        gain_all = lax.all_gather(gain_blk, "tx", axis=0, tiled=True)
        x_row = lax.all_gather(x_blk, "tx", axis=1, tiled=True)
        x_all = lax.all_gather(x_row, "ty", axis=0, tiled=True)
        dy_row = lax.all_gather(dy_blk, "tx", axis=1, tiled=True)
        dy_all = lax.all_gather(dy_row, "ty", axis=0, tiled=True)

        xf = x_all.astype(jnp.float32)
        mean_x = jnp.sum(xf, axis=1, keepdims=True) / d_model
        mean_s = jnp.sum(xf * xf, axis=1, keepdims=True) / d_model
        inv_all = lax.rsqrt(mean_s - mean_x * mean_x + LN_EPS)
        h_all = (gain_all * ((xf - mean_x) * inv_all)).astype(jnp.bfloat16)
        my_row = lax.axis_index("ty") * rows
        mu = lax.dynamic_slice_in_dim(mean_x, my_row, rows, 0)
        inv_std = lax.dynamic_slice_in_dim(inv_all, my_row, rows, 0)
        x_float = x_blk.astype(jnp.float32)
        x_hat = (x_float - mu) * inv_std

        u = jnp.dot(h_all, w_gate_all, preferred_element_type=jnp.float32)
        v = jnp.dot(h_all, w_up_all, preferred_element_type=jnp.float32)
        sig = jax.nn.sigmoid(u)
        swish = u * sig
        act = (swish * v).astype(jnp.bfloat16)
        d_act = contract_cols(dy_all, w_down_all)
        d_gate = (d_act * v * sig * (1.0 + u * (1.0 - sig))).astype(jnp.bfloat16)
        d_up = (d_act * swish).astype(jnp.bfloat16)

        def pair(a):
            return lax.all_gather(a, "tx", axis=1, tiled=True, axis_index_groups=CHIP)

        act_all, d_gate_all, d_up_all = pair(act), pair(d_gate), pair(d_up)
        mlp_out = lax.psum_scatter(jnp.dot(act_all, w_down_blk, preferred_element_type=jnp.float32),
                                   "ty", scatter_dimension=0, tiled=True)
        y_blk = (x_float + mlp_out).astype(jnp.bfloat16)
        d_hnorm = lax.psum_scatter(contract_cols(d_gate_all, w_gate_blk) + contract_cols(d_up_all, w_up_blk),
                                   "ty", scatter_dimension=0, tiled=True)
        h_my = lax.dynamic_slice_in_dim(h_all, tx * cols, cols, 1)
        dy_my = lax.dynamic_slice_in_dim(dy_all, tx * cols, cols, 1)
        dw_down_blk = contract_rows(act_all, dy_my)
        dw_gate_blk = contract_rows(h_my, d_gate_all)
        dw_up_blk = contract_rows(h_my, d_up_all)
        e = d_hnorm * gain_blk
        bwd_stats = lax.psum(jnp.stack([jnp.sum(e, axis=1), jnp.sum(e * x_hat, axis=1)]), "tx") / d_model
        dx_ln = inv_std * (e - bwd_stats[0][:, None] - x_hat * bwd_stats[1][:, None])
        dx_blk = (dy_blk.astype(jnp.float32) + dx_ln).astype(jnp.bfloat16)
        d_gain_blk = lax.psum(jnp.sum(d_hnorm * x_hat, axis=0), "ty")
        return (y_blk, dx_blk, dw_gate_blk, dw_up_blk, dw_down_blk, d_gain_blk)

    return jax.shard_map(
        local_step, mesh=mesh,
        in_specs=(P("ty", "tx"), P("ty", "tx"), P("tx"), P("tx", "ty"), P("tx", "ty"), P("ty", "tx")),
        out_specs=(P("ty", "tx"), P("ty", "tx"), P("tx", "ty"), P("tx", "ty"), P("ty", "tx"), P("tx")),
        check_vma=False)
```

time: 1340 us -> 880 us (0.66)
  waiting for transfers between devices: 1120 us -> 637 us
  matrix products: 143 us -> 173 us
    reduce_scatter x3 -> x0, waiting for transfers between devices: 673 us -> none  [the longest x1 230 us: local_step(): lax.psum_scatter(jnp.dot(h_all, w_gate_blk, preferred_element_type=jnp.fl...]
    all_gather x5 -> x10, waiting for transfers between devices: 347 us -> 537 us  [the longest x1 155 us: local_step(): dy_all = lax.all_gather(dy_row, 'ty', axis=0, tiled=True)]
    dot_general x3, matrix products: 51.2 us -> 69.1 us  [contract_cols(): lax.dot_general(left_op, right_op, (((1,), (1,)), ((), ())), preferred_el...]
  transfers between devices with their start and end apart: 10 -> 12, of which waited for: 10 -> 12; matrix products, arithmetic and copies ran while one was open for 11% -> 18% of each run, Pallas kernels for 0% -> 0%
where the time goes in v1:
time: 880 us; the launch traced here: 873 us
  waiting for transfers between devices  637 us (72%)
  matrix products  173 us (20%)
  other arithmetic  24.1 us (3%)
  blocking collectives  20.9 us (2%)
  between operations  14.6 us (2%)
    all_gather x1, waiting for transfers between devices, local_step(): dy_all = lax.all_gather(dy_row, 'ty', axis=0, tiled=True)  155 us
    all_gather x1, waiting for transfers between devices, local_step(): x_all = lax.all_gather(x_row, 'ty', axis=0, tiled=True)  150 us
    dot_general x3, matrix products, contract_cols(): lax.dot_general(left_op, right_op, (((1,), (1,)), ((), ())), preferred_el...  69.1 us
    reduce_scatter x1, waiting for transfers between devices, local_step(): lax.psum_scatter(jnp.dot(act_all, w_down_blk, preferred_element_type=jnp....  66.9 us
    all_gather x3, waiting for transfers between devices, pair(): return lax.all_gather(a, 'tx', axis=1, tiled=True, axis_index_groups=CHIP)  56.1 us
    dot_general x3, matrix products, contract_rows(): lax.dot_general(left_op, right_op, (((0,), (0,)), ((), ())), preferred_el...  42.5 us
    all_gather x1, waiting for transfers between devices, local_step(): w_up_all = pick(lax.all_gather(w_up_blk, 'tx', axis=0, tiled=True))  37.9 us
    all_gather x1, waiting for transfers between devices, local_step(): x_row = lax.all_gather(x_blk, 'tx', axis=1, tiled=True)  36.1 us
  transfers between devices with their start and end apart: 12, of which 12 were waited for; matrix products, arithmetic and copies ran while one was open for 18% of the time, Pallas kernels for 0%

profile of v1, /device:TPU:0, one launch (start us, length us, event | category | flops | bytes accessed | tf_op | source)
XLA Modules:
  0.0 873.2 jit_solution(12887324970116604384)
XLA Ops:
  7.2 0.0 copy-start.7
  7.2 0.0 all-gather.12.cloned.1.call-start
  7.2 0.7 all-gather.12.cloned.1.call-update
  7.9 0.0 all-gather.24.cloned.1.call-start
  8.0 0.7 all-gather.24.cloned.1.call-update
  8.7 0.0 all-gather.14.cloned.1.call-start
  8.7 36.1 %all-gather.12.cloned.1.call-done = bf16[1024,2048]{1,0:T(8,128)(2,1)} async-done(((bf16[1024,512]{1,0:T(8,128)(2,1)}), bf16[1024,2048]{1,0:T(8,128)(2,1)}) %all-gather.12.cloned.1.call-update) | async-done | bytes 4194320 | tf_op jit(solution)/shard_map/all_gather | solution.py:36
  44.8 0.0 all-gather.14.cloned.1.call-update
  44.8 0.0 all-gather.18.cloned.1.call-start
  44.9 0.5 all-gather.18.cloned.1.call-update
  45.4 0.0 all-gather.16.cloned.1.call-start
  45.4 0.5 all-gather.16.cloned.1.call-update
  46.0 0.0 all-gather.22.cloned.1.call-start
  46.0 0.5 all-gather.22.cloned.1.call-update
  46.6 0.0 all-gather.26.cloned.1.call-start
  46.6 32.2 %all-gather.24.cloned.1.call-done = bf16[1024,2048]{1,0:T(8,128)(2,1)} async-done(((bf16[1024,512]{1,0:T(8,128)(2,1)}), bf16[1024,2048]{1,0:T(8,128)(2,1)}) %all-gather.24.cloned.1.call-update) | async-done | bytes 4194320 | tf_op jit(solution)/shard_map/all_gather | solution.py:38
  78.8 0.0 all-gather.26.cloned.1.call-update
  78.8 0.0 all-gather.28.cloned.1.call-start
  78.9 5.2 all-gather
  84.0 150.2 %all-gather.14.cloned.1.call-done = bf16[4096,2048]{1,0:T(8,128)(2,1)} async-done(((bf16[1024,2048]{1,0:T(8,128)(2,1)}), bf16[4096,2048]{1,0:T(8,128)(2,1)}) %all-gather.14.cloned.1.call-update) | async-done | bytes 16777232 | tf_op jit(solution)/shard_map/all_gather | solution.py:37
  234.3 8.5 convert_reduce_fusion
  242.8 0.0 copy-start.5
  242.8 0.0 copy-start.6
  242.8 0.6 copy-done.5
  243.4 0.0 copy-done.6
  243.4 1.6 copy-done
  245.0 9.4 %fusion.2 = bf16[4096,2048]{1,0:T(8,128)(2,1)} fusion(bf16[4096,2048]{1,0:T(8,128)(2,1)S(1)} %copy-done, f32[4096]{0:T(1024)S(1)} %get-tuple-element.17, f32[4096]{0:T(1024)S(1)} %get-tuple-element.16, f32[2048]{0:T(1024)S(1)} %bitcast.29), kind=kLoop, calls=%fused_computation.5 | loop fusion | flops 41943040 | bytes 33595392 | tf_op jit(solution)/shard_map/convert_element_type | solution.py:45
  254.4 37.9 %all-gather.18.cloned.1.call-done = bf16[2048,2048]{1,0:T(8,128)(2,1)} async-done(((bf16[512,2048]{1,0:T(8,128)(2,1)}), bf16[2048,2048]{1,0:T(8,128)(2,1)}) %all-gather.18.cloned.1.call-update) | async-done | bytes 8388624 | tf_op jit(solution)/shard_map/all_gather | solution.py:33
  292.3 23.4 %fusion.13 = f32[4096,1024]{1,0:T(8,128)} fusion(bf16[4096,2048]{1,0:T(8,128)(2,1)} %fusion.2, bf16[2048,2048]{1,0:T(8,128)(2,1)} %all-gather.18.cloned.1.call-done, s32[]{:T(128)S(6)} %select_n.6), kind=kOutput, calls=%fused_computation.21 | convolution fusion | flops 17179869184 | bytes 37748740 | tf_op jit(solution)/shard_map/dot_general | solution.py:53
  315.7 34.6 %all-gather.16.cloned.1.call-done = bf16[2048,2048]{1,0:T(8,128)(2,1)} async-done(((bf16[512,2048]{1,0:T(8,128)(2,1)}), bf16[2048,2048]{1,0:T(8,128)(2,1)}) %all-gather.16.cloned.1.call-update) | async-done | bytes 8388624 | tf_op jit(solution)/shard_map/all_gather | solution.py:32
  350.4 23.4 %fusion.15 = f32[4096,1024]{1,0:T(8,128)} fusion(bf16[4096,2048]{1,0:T(8,128)(2,1)} %fusion.2, bf16[2048,2048]{1,0:T(8,128)(2,1)} %all-gather.16.cloned.1.call-done, s32[]{:T(128)S(6)} %select_n.6), kind=kOutput, calls=%fused_computation.23 | convolution fusion | flops 17179869184 | bytes 37748740 | tf_op jit(solution)/shard_map/dot_general | solution.py:52
  373.8 34.6 %all-gather.22.cloned.1.call-done = bf16[2048,2048]{1,0:T(8,128)(2,1)} async-done(((bf16[2048,512]{1,0:T(8,128)(2,1)}), bf16[2048,2048]{1,0:T(8,128)(2,1)}) %all-gather.22.cloned.1.call-update) | async-done | bytes 8388624 | tf_op jit(solution)/shard_map/all_gather | solution.py:34
  408.4 155.5 %all-gather.26.cloned.1.call-done = bf16[4096,2048]{1,0:T(8,128)(2,1)} async-done(((bf16[1024,2048]{1,0:T(8,128)(2,1)}), bf16[4096,2048]{1,0:T(8,128)(2,1)}) %all-gather.26.cloned.1.call-update) | async-done | bytes 16777232 | tf_op jit(solution)/shard_map/all_gather | solution.py:39
  563.9 35.1 %fusion.7 = (bf16[4096,1024]{1,0:T(8,128)(2,1)}, bf16[4096,1024]{1,0:T(8,128)(2,1)}, bf16[4096,1024]{1,0:T(8,128)(2,1)}) fusion(f32[4096,1024]{1,0:T(8,128)} %fusion.15, f32[4096,1024]{1,0:T(8,128)} %fusion.13, bf16[4096,2048]{1,0:T(8,128)(2,1)} %all-gather.26.cloned.1.call-done, bf16[2048,2048]{1,0:T(8,128)(2,1)} %all-gather.22.cloned.1.call-done, ...), kind=kOutput, calls=%fused_computation.12 | convolution fusion | flops 17242783744 | bytes 79691776 | tf_op jit(solution)/shard_map/dot_general | solution.py:15
  599.0 0.0 all-gather.28.cloned.1.call-update
  599.0 0.0 all-gather.30.cloned.1.call-start
  599.1 0.0 copy-start.3
  599.1 0.7 all-gather.30.cloned.1.call-update
  599.8 0.0 all-gather.20.cloned.1.call-start
  599.8 0.5 all-gather.20.cloned.1.call-update
  600.3 0.0 reduce-scatter.5.cloned.1.call-start
  600.4 27.5 %all-gather.28.cloned.1.call-done = bf16[4096,2048]{1,0:T(8,128)(2,1)} async-done(((bf16[4096,1024]{1,0:T(8,128)(2,1)}), bf16[4096,2048]{1,0:T(8,128)(2,1)}) %all-gather.28.cloned.1.call-update) | async-done | bytes 16777232 | tf_op jit(solution)/shard_map/all_gather | solution.py:62
  627.9 15.1 %fusion.40 = f32[4096,512]{1,0:T(8,128)} fusion(bf16[4096,2048]{1,0:T(8,128)(2,1)} %all-gather.28.cloned.1.call-done, bf16[512,2048]{1,0:T(8,128)(2,1)S(1)} %copy-done.3), kind=kOutput, calls=%fused_computation.55 | convolution fusion | flops 8589934592 | bytes 27262976 | tf_op jit(solution)/shard_map/dot_general | solution.py:15
  643.0 16.4 %all-gather.30.cloned.1.call-done = bf16[4096,2048]{1,0:T(8,128)(2,1)} async-done(((bf16[4096,1024]{1,0:T(8,128)(2,1)}), bf16[4096,2048]{1,0:T(8,128)(2,1)}) %all-gather.30.cloned.1.call-update) | async-done | bytes 16777232 | tf_op jit(solution)/shard_map/all_gather | solution.py:62
  659.3 18.9 %convolution_add_fusion = f32[4096,512]{1,0:T(8,128)} fusion(f32[4096,512]{1,0:T(8,128)} %fusion.40, bf16[4096,2048]{1,0:T(8,128)(2,1)} %all-gather.30.cloned.1.call-done, bf16[512,2048]{1,0:T(8,128)(2,1)} %param.10), kind=kOutput, calls=%fused_computation.16 | convolution fusion | flops 8592031744 | bytes 35651584 | tf_op jit(solution)/shard_map/dot_general | solution.py:15
  678.3 0.0 reduce-scatter.5.cloned.1.call-update
  678.3 0.0 reduce-scatter.3.cloned.1.call-start
  678.3 12.3 %all-gather.20.cloned.1.call-done = bf16[4096,2048]{1,0:T(8,128)(2,1)} async-done(((bf16[4096,1024]{1,0:T(8,128)(2,1)}), bf16[4096,2048]{1,0:T(8,128)(2,1)}) %all-gather.20.cloned.1.call-update) | async-done | bytes 16777232 | tf_op jit(solution)/shard_map/all_gather | solution.py:62
  690.6 14.6 %fusion.39 = f32[4096,512]{1,0:T(8,128)} fusion(bf16[4096,2048]{1,0:T(8,128)(2,1)} %all-gather.20.cloned.1.call-done, bf16[2048,512]{1,0:T(8,128)(2,1)S(1)} %copy-done.4), kind=kOutput, calls=%fused_computation.54 | convolution fusion | flops 8589934592 | bytes 27262976 | tf_op jit(solution)/shard_map/dot_general | solution.py:65
  705.2 0.0 reduce-scatter.3.cloned.1.call-update
  705.2 0.7 dynamic-slice.3
  705.9 0.7 dynamic-slice.4
  706.6 15.1 %fusion.9 = f32[2048,512]{1,0:T(8,128)} fusion(bf16[4096,2048]{1,0:T(8,128)(2,1)} %all-gather.20.cloned.1.call-done, bf16[4096,2048]{1,0:T(8,128)(2,1)} %all-gather.26.cloned.1.call-done, s32[]{:T(128)S(6)} %select_n.15), kind=kOutput, calls=%fused_computation.17 | convolution fusion | flops 8589934592 | bytes 25165828 | tf_op jit(solution)/shard_map/dot_general | solution.py:11
  721.7 15.1 %fusion.19 = f32[512,2048]{1,0:T(8,128)} fusion(bf16[4096,2048]{1,0:T(8,128)(2,1)} %all-gather.28.cloned.1.call-done, bf16[4096,2048]{1,0:T(8,128)(2,1)} %fusion.2, s32[]{:T(128)S(6)} %select_n.15), kind=kOutput, calls=%fused_computation.27 | convolution fusion | flops 8589934592 | bytes 25165828 | tf_op jit(solution)/shard_map/dot_general | solution.py:11
  736.8 0.0 copy-start.1
  736.8 0.0 copy-start.8
  736.9 0.0 copy-start.2
  736.9 12.3 %fusion.17 = f32[512,2048]{1,0:T(8,128)} fusion(bf16[4096,2048]{1,0:T(8,128)(2,1)S(1)} %bitcast.36, bf16[4096,2048]{1,0:T(8,128)(2,1)} %fusion.2, s32[]{:T(128)S(6)} %select_n.15), kind=kOutput, calls=%fused_computation.25 | convolution fusion | flops 8589934592 | bytes 25165828 | tf_op jit(solution)/shard_map/dot_general | solution.py:11
  749.2 28.1 %reduce-scatter.5.cloned.1.call-done = f32[1024,512]{1,0:T(8,128)} async-done(((f32[4096,512]{1,0:T(8,128)}), f32[1024,512]{1,0:T(8,128)}) %reduce-scatter.5.cloned.1.call-update) | async-done | bytes 2097168 | tf_op jit(solution)/shard_map/reduce_scatter | solution.py:68
  777.2 2.6 fusion.31
  779.8 9.6 %psum.15 = f32[512]{0:T(512)} all-reduce(f32[512]{0:T(512)S(1)} %get-tuple-element.8), channel_id=1, replica_groups=mesh['ty'=4,'tx'=4] {'ty'}, use_global_device_ids=true, to_apply=%region_8.0 | all-reduce | flops 512 | bytes 4096 | tf_op jit(solution)/shard_map/psum | solution.py:79
  789.4 6.2 psum.14
  795.6 66.9 %reduce-scatter.3.cloned.1.call-done = f32[1024,512]{1,0:T(8,128)} async-done(((f32[4096,512]{1,0:T(8,128)}), f32[1024,512]{1,0:T(8,128)}) %reduce-scatter.3.cloned.1.call-update) | async-done | bytes 2097168 | tf_op jit(solution)/shard_map/reduce_scatter | solution.py:65
  862.5 3.6 fusion.30
  (21 shorter events, 0.1 us)
Async XLA Ops:
  7.2 71.7 %copy-start.7 = (f32[512]{0:T(512)S(1)}, f32[512]{0:T(512)}, u32[]{:S(2)}) copy-start(f32[512]{0:T(512)} %param.8) | copy-start | bytes 6148
  7.2 37.6 %all-gather.12.cloned.1.call-start = ((), (), s32[]{:S(2)}) async-start(), calls=%async_computation.2 | async-start | bytes 5242880 | tf_op jit(solution)/shard_map/all_gather | solution.py:36
  7.9 70.9 %all-gather.24.cloned.1.call-start = ((), (), s32[]{:S(2)}) async-start(), calls=%async_computation.9 | async-start | bytes 5242880 | tf_op jit(solution)/shard_map/all_gather | solution.py:38
  8.7 225.6 %all-gather.14.cloned.1.call-start = ((), (), s32[]{:S(2)}) async-start(), calls=%async_computation.3 | async-start | bytes 20971520 | tf_op jit(solution)/shard_map/all_gather | solution.py:37
  44.8 247.5 %all-gather.18.cloned.1.call-start = ((), (), s32[]{:S(2)}) async-start(), calls=%async_computation.5 | async-start | bytes 10485760 | tf_op jit(solution)/shard_map/all_gather | solution.py:33
  45.4 305.0 %all-gather.16.cloned.1.call-start = ((), (), s32[]{:S(2)}) async-start(), calls=%async_computation.4 | async-start | bytes 10485760 | tf_op jit(solution)/shard_map/all_gather | solution.py:32
  46.0 362.4 %all-gather.22.cloned.1.call-start = ((), (), s32[]{:S(2)}) async-start(), calls=%async_computation.8 | async-start | bytes 10485760 | tf_op jit(solution)/shard_map/all_gather | solution.py:34
  46.6 517.4 %all-gather.26.cloned.1.call-start = ((), (), s32[]{:S(2)}) async-start(), calls=%async_computation.10 | async-start | bytes 20971520 | tf_op jit(solution)/shard_map/all_gather | solution.py:39
  78.8 549.1 %all-gather.28.cloned.1.call-start = ((), (), s32[]{:S(2)}) async-start(), calls=%async_computation.11 | async-start | bytes 25165824 | tf_op jit(solution)/shard_map/all_gather | solution.py:62
  234.3 10.8 %copy-start = (bf16[4096,2048]{1,0:T(8,128)(2,1)S(1)}, bf16[4096,2048]{1,0:T(8,128)(2,1)}, u32[]{:S(2)}) copy-start(bf16[4096,2048]{1,0:T(8,128)(2,1)} %all-gather.14.cloned.1.call-done) | copy-start | bytes 50331652
  242.8 0.6 copy-start.5
  242.8 0.6 copy-start.6
  599.0 60.3 %all-gather.30.cloned.1.call-start = ((), (), s32[]{:S(2)}) async-start(), calls=%async_computation.12 | async-start | bytes 25165824 | tf_op jit(solution)/shard_map/all_gather | solution.py:62
  599.1 28.8 %copy-start.3 = (bf16[512,2048]{1,0:T(8,128)(2,1)S(1)}, bf16[512,2048]{1,0:T(8,128)(2,1)}, u32[]{:S(2)}) copy-start(bf16[512,2048]{1,0:T(8,128)(2,1)} %param.9) | copy-start | bytes 6291460
  599.8 90.9 %all-gather.20.cloned.1.call-start = ((), (), s32[]{:S(2)}) async-start(), calls=%async_computation.6 | async-start | bytes 25165824 | tf_op jit(solution)/shard_map/all_gather | solution.py:62
  600.3 176.9 %reduce-scatter.5.cloned.1.call-start = ((), (), s32[]{:S(2)}) async-start(), calls=%async_computation.13 | async-start | bytes 10485760 | tf_op jit(solution)/shard_map/reduce_scatter | solution.py:68
  678.2 12.4 %copy-start.4 = (bf16[2048,512]{1,0:T(8,128)(2,1)S(1)}, bf16[2048,512]{1,0:T(8,128)(2,1)}, u32[]{:S(2)}) copy-start(bf16[2048,512]{1,0:T(8,128)(2,1)} %param.11) | copy-start | bytes 6291460
  678.3 184.3 %reduce-scatter.3.cloned.1.call-start = ((), (), s32[]{:S(2)}) async-start(), calls=%async_computation.7 | async-start | bytes 10485760 | tf_op jit(solution)/shard_map/reduce_scatter | solution.py:65
  706.6 30.2 %slice-start = ((s8[16777216]{0:T(1024)(128)(4,1)}), s8[4194304]{0:T(1024)(128)(4,1)S(1)}, s32[]{:S(2)}) async-start(s8[16777216]{0:T(1024)(128)(4,1)} %bitcast.35), calls=%async_computation.14 | async-start | bytes 8388608
  706.6 30.2 %slice-start.1 = ((s8[16777216]{0:T(1024)(128)(4,1)}), s8[4194304]{0:T(1024)(128)(4,1)S(1)}, s32[]{:S(2)}) async-start(s8[16777216]{0:T(1024)(128)(4,1)} %bitcast.35), calls=%async_computation.15 | async-start | bytes 8388608
  721.7 15.1 %slice-start.2 = ((s8[16777216]{0:T(1024)(128)(4,1)}), s8[4194304]{0:T(1024)(128)(4,1)S(1)}, s32[]{:S(2)}) async-start(s8[16777216]{0:T(1024)(128)(4,1)} %bitcast.35), calls=%async_computation.16 | async-start | bytes 8388608
  721.7 15.1 %slice-start.3 = ((s8[16777216]{0:T(1024)(128)(4,1)}), s8[4194304]{0:T(1024)(128)(4,1)S(1)}, s32[]{:S(2)}) async-start(s8[16777216]{0:T(1024)(128)(4,1)} %bitcast.35), calls=%async_computation.17 | async-start | bytes 8388608
  736.8 40.4 %copy-start.1 = (bf16[1024,512]{1,0:T(8,128)(2,1)S(1)}, bf16[1024,512]{1,0:T(8,128)(2,1)}, u32[]{:S(2)}) copy-start(bf16[1024,512]{1,0:T(8,128)(2,1)} %param.6) | copy-start | bytes 3145732
  736.8 40.4 %copy-start.8 = (f32[512]{0:T(512)S(1)}, f32[512]{0:T(512)}, u32[]{:S(2)}) copy-start(f32[512]{0:T(512)} %param.8) | copy-start | bytes 6148
  736.9 125.7 %copy-start.2 = (bf16[1024,512]{1,0:T(8,128)(2,1)S(1)}, bf16[1024,512]{1,0:T(8,128)(2,1)}, u32[]{:S(2)}) copy-start(bf16[1024,512]{1,0:T(8,128)(2,1)} %param.7) | copy-start | bytes 3145732
Sparse Core Ops, SparseCore 0:
  9.5 35.2 all-gather.11
  46.3 32.3 all-gather.23
  80.6 153.6 all-gather.13
  235.7 56.6 all-gather.17
  293.7 56.6 all-gather.15
  351.8 56.6 all-gather.21
  410.2 153.6 all-gather.25
  599.1 28.6 all-gather.27
  629.4 29.8 all-gather.29
  660.7 29.8 all-gather.19
  693.7 83.5 reduce-scatter.4
  780.1 82.3 reduce-scatter.2

commit v2 on v0

v2 whole, which is shorter than its diff:
```python
import jax
import jax.numpy as jnp
from jax import lax
from jax.experimental import pallas as pl
from jax.experimental.pallas import tpu as pltpu
from jax.sharding import PartitionSpec as P

LN_EPS = 1e-6
MESH = pl.DeviceIdType.MESH
BF16 = jnp.bfloat16
F32 = jnp.float32
STEPS = 8
ROWS = 128
TOK = 4 * ROWS
DQ = 512
DM = 4 * DQ
FB = 2048
FH = FB // 2
NT = (((1,), (1,)), ((), ()))
X, YA, YB, YBF, ZA, ZB, ZAF, C0, C1 = range(9)


def kernel(x_ref, dy_ref, g_ref, wg_ref, wu_ref, wd_ref,
           y_ref, dx_ref, dw1_ref, dw3_ref, dw2_ref, dg_ref,
           xg, dyg, hg, ug, vg, ag, dug, dvg, rcv1, rcv2,
           w1g, w3g, w2g, w1o, w3o, w2o, acc1, acc3, acc2, b0, b1, dyb, ab, ub, vb,
           hq, hqt, dyq, dyqt, xown, dyown, part, r1, r2, gfull, gsrc, st, stall, dhs, yst,
           pst, pstr, dgs, dgr,
           gs, gr, ws, wr, ggs, ggr, cs, cr, rss, rsr, ss, sr, dgss, dgsr, loc, hst, ust, qst, pstm, ast, hld, uld, ald,
           dld, xld, rld, yld, wst):
    ty = lax.axis_index("ty")
    tx = lax.axis_index("tx")
    y = ty % 2
    z = ty // 2
    c = tx % 2
    tx2 = (tx + 2) % 4
    ty_y = ty + 1 - 2 * y
    ty_z = (ty + 2) % 4
    XP = (ty, tx2)
    CP = (ty, tx + 1 - 2 * c)
    XC = (ty, tx2 + 1 - 2 * c)
    YP = (ty_y, tx)
    ZP = (ty_z, tx)
    YZ = (ty_z + 1 - 2 * y, tx)

    def rc(src, dst, s, r, dev):
        return pltpu.make_async_remote_copy(src_ref=src, dst_ref=dst, send_sem=s, recv_sem=r,
                                            device_id=dev, device_id_type=MESH)

    def lc(src, dst, s):
        return pltpu.make_async_copy(src, dst, s)

    def row(j):
        return pl.ds(pl.multiple_of(j * ROWS, ROWS), ROWS)

    def qcol(q):
        return pl.ds(pl.multiple_of(q * DQ, DQ), DQ)

    def hcol(h):
        return pl.ds(pl.multiple_of(h * FH, FH), FH)

    def gcopy(arr, kind, s):
        own, buf = ((x_ref, xg), (dy_ref, dyg))[arr]
        a, b = gs.at[arr, kind, s], gr.at[arr, kind, s]
        mine = buf.at[tx, s, row(ty)]
        other = buf.at[tx2, s, row(ty)]
        if kind == X:
            return rc(own.at[s], mine, a, b, XP)
        if kind == YA:
            return rc(own.at[s], mine, a, b, YP)
        if kind == ZA:
            return rc(own.at[s], mine, a, b, ZP)
        if kind == YB:
            return rc(other, other, a, b, YP)
        if kind == ZB:
            return rc(other, other, a, b, ZP)
        if kind == ZAF:
            blk = buf.at[tx, s, row(ty_y)]
            return rc(blk, blk, a, b, ZP)
        if kind == YBF:
            blk = buf.at[tx2, s, row(ty_z)]
            return rc(blk, blk, a, b, YP)
        blk = buf.at[tx if kind == C0 else tx2, s]
        return rc(blk, blk, a, b, CP)

    def loop(n, f):
        def body(s, carry):
            f(s)
            return carry
        lax.fori_loop(0, n, body, 0)

    def wcopy(w, k):
        dev, h = ((XP, c), (XC, 1 - c), (CP, 1 - c))[k]
        a, b = ws.at[w, k], wr.at[w, k]
        if w < 2:
            return rc((wg_ref, wu_ref)[w].at[:, hcol(h)], (w1g, w3g)[w].at[qcol(tx), :], a, b, dev)
        return rc(wd_ref.at[hcol(h), :], w2g.at[:, qcol(tx)], a, b, dev)

    def gaincopy(k):
        return rc(gsrc, gfull.at[:, qcol(tx)], ggs.at[k], ggr.at[k], (XP, XC, CP)[k])

    gsrc[...] = jnp.broadcast_to(g_ref[...], (8, DQ))
    barrier = pltpu.get_barrier_semaphore()
    for dev in (XP, CP, XC, YP, ZP, YZ):
        pl.semaphore_signal(barrier, inc=1, device_id=dev, device_id_type=MESH)
    own_in = [lc(x_ref, xown, loc.at[0]), lc(dy_ref, dyown, loc.at[1])]
    w_in = [lc(wg_ref, w1o, loc.at[2]), lc(wu_ref, w3o, loc.at[3]), lc(wd_ref, w2o, loc.at[4]),
            lc(wg_ref.at[:, hcol(c)], w1g.at[qcol(tx), :], loc.at[5]),
            lc(wu_ref.at[:, hcol(c)], w3g.at[qcol(tx), :], loc.at[6]),
            lc(wd_ref.at[hcol(c), :], w2g.at[:, qcol(tx)], loc.at[7])]
    for d in own_in:
        d.start()
    pl.semaphore_wait(barrier, 6)

    for k in range(3):
        gaincopy(k).start()
    loop(STEPS, lambda s: gcopy(0, X, s).start())

    def send_a(s):
        gcopy(0, YA, s).start()
        gcopy(0, ZA, s).start()
    loop(STEPS, send_a)
    for w in range(2):
        for k in range(3):
            wcopy(w, k).start()
    loop(STEPS, lambda s: gcopy(1, X, s).start())
    for k in range(3):
        wcopy(2, k).start()
    for d in w_in:
        d.start()
    for d in own_in:
        d.wait()
    own_out = [lc(xown, xg.at[tx, :, row(ty)], loc.at[0]), lc(dyown, dyg.at[tx, :, row(ty)], loc.at[1])]
    for d in own_out:
        d.start()
    gfull[:, qcol(tx)] = gsrc[...]

    def l1(arr, s):
        gcopy(arr, X, s).wait_recv()
        gcopy(arr, YB, s).start()
        gcopy(arr, ZB, s).start()

    def l1f(arr, s):
        gcopy(arr, YA, s).wait_recv()
        gcopy(arr, ZAF, s).start()

    def l2(arr, s):
        gcopy(arr, ZB, s).wait_recv()
        gcopy(arr, YBF, s).start()

    def l3(arr, s):
        gcopy(arr, ZA, s).wait_recv()
        gcopy(arr, ZAF, s).wait_recv()
        gcopy(arr, C0, s).start()
        gcopy(arr, YB, s).wait_recv()
        gcopy(arr, YBF, s).wait_recv()
        gcopy(arr, C1, s).start()

    def first(s):
        l1(0, s)
        l1f(0, s)
    loop(STEPS, first)
    loop(STEPS, lambda s: l2(0, s))

    def send_dya(s):
        gcopy(1, YA, s).start()
        gcopy(1, ZA, s).start()
    loop(STEPS, send_dya)
    for d in own_out:
        d.wait()
    for d in w_in:
        d.wait()
    for k in range(3):
        gaincopy(k).wait_recv()
    loop(STEPS, lambda s: l3(0, s))

    def block_loads(arr, s, dst, sem):
        buf = (xg, dyg)[arr]
        return [lc(buf.at[q, s], dst.at[:, q * DQ:(q + 1) * DQ], sem.at[q]) for q in range(4)]

    def wait_block(arr, s):
        gcopy(arr, C0, s).wait_recv()
        gcopy(arr, C1, s).wait_recv()

    xs, hb = b1.at[0], b1.at[1]

    def h_store(s):
        return lc(hb, hg.at[s], hst.at[0])

    def u_store(s):
        return lc(acc2.at[:, hcol(s % 2)], ug.at[s], ust.at[s % 2])

    wait_block(0, 0)
    for d in block_loads(0, 0, xs, xld):
        d.start()
    for k in range(3):
        wcopy(0, k).wait_recv()

    def pass1(s):
        for d in block_loads(0, s, xs, xld):
            d.wait()

        @pl.when(s >= 1)
        def _():
            h_store(s - 1).wait()

        def chunk(i):
            rr = pl.ds(pl.multiple_of(i * 64, 64), 64)
            xf = xs[rr, :].astype(F32)
            mu = jnp.sum(xf, axis=1, keepdims=True) * (1.0 / DM)
            sq = jnp.sum(xf * xf, axis=1, keepdims=True) * (1.0 / DM)
            inv = lax.rsqrt(sq - mu * mu + LN_EPS)
            hb[rr, :] = (gfull[0:1, :] * ((xf - mu) * inv)).astype(BF16)
            lane = lax.broadcasted_iota(jnp.int32, (64, 128), 1)
            stall[rr, :] = jnp.where(lane == 0, mu, inv)
        loop(TOK // 64, chunk)
        st[s] = stall[row(ty), :]
        h_store(s).start()

        @pl.when(s < STEPS - 1)
        def _():
            wait_block(0, s + 1)
            for d in block_loads(0, s + 1, xs, xld):
                d.start()

        @pl.when(s >= 2)
        def _():
            u_store(s - 2).wait()
        acc2[:, hcol(s % 2)] = jnp.dot(hb[...], w1g[...], preferred_element_type=F32)
        u_store(s).start()
        l1f(1, s)
    loop(STEPS, pass1)
    h_store(STEPS - 1).wait()
    u_store(STEPS - 2).wait()
    u_store(STEPS - 1).wait()

    def rs_copy(kind, n):
        slot = n % 3
        a, b = rss.at[kind, n], rsr.at[kind, n]
        if kind == 0:
            return rc(part.at[slot, 0, 1 - y], rcv1.at[n, 0], a, b, YP)
        if kind == 1:
            return rc(part.at[slot, 1, 1 - z], rcv1.at[n, 1], a, b, ZP)
        if kind == 2:
            return rc(part.at[slot, 0, y, 1 - z], rcv2.at[n, 0], a, b, ZP)
        return rc(part.at[slot, 1, z, 1 - y], rcv2.at[n, 1], a, b, YP)

    def rs_put(n, val):
        slot = n % 3
        for j in range(4):
            part[slot, 0, j % 2, j // 2] = val[j * ROWS:(j + 1) * ROWS, 0:256]
            part[slot, 1, j // 2, j % 2] = val[j * ROWS:(j + 1) * ROWS, 256:512]

    def rs_first(n):
        rs_copy(0, n).start()
        rs_copy(1, n).start()

    def rs_loads(K):
        @pl.when((K >= 2) & (K <= 17))
        def _():
            rs_copy(0, K - 2).wait_recv()
            rs_copy(1, K - 2).wait_recv()
            lc(rcv1.at[K - 2], r1, rld.at[0]).start()

        @pl.when((K >= 3) & (K <= 18))
        def _():
            rs_copy(2, K - 3).wait_recv()
            rs_copy(3, K - 3).wait_recv()
            lc(rcv2.at[K - 3], r2, rld.at[1]).start()

    def y_store(n):
        return lc(yst.at[n % 2], y_ref.at[n], yld.at[n % 2])

    def rs_proc(K):
        @pl.when((K >= 2) & (K <= 17))
        def _():
            n = K - 2
            slot = n % 3
            lc(rcv1.at[n], r1, rld.at[0]).wait()
            for k in range(2):
                part[slot, 0, y, k] += r1[0, k]
                part[slot, 1, z, k] += r1[1, k]
            rs_copy(2, n).start()
            rs_copy(3, n).start()

        @pl.when((K >= 3) & (K <= 18))
        def _():
            n = K - 3
            slot = n % 3
            lc(rcv2.at[n], r2, rld.at[1]).wait()
            for k in range(4):
                rs_copy(k, n).wait_send()

            @pl.when(n < 8)
            def _():
                @pl.when(n >= 2)
                def _():
                    y_store(n - 2).wait()
                yst[n % 2, :, 0:256] = (xown[n, :, 0:256].astype(F32) + (part[slot, 0, y, z] + r2[0])).astype(BF16)
                yst[n % 2, :, 256:512] = (xown[n, :, 256:512].astype(F32) + (part[slot, 1, z, y] + r2[1])).astype(BF16)
                y_store(n).start()

            @pl.when(n >= 8)
            def _():
                s = n - 8
                dhs[s, :, 0:256] = part[slot, 0, y, z] + r2[0]
                dhs[s, :, 256:512] = part[slot, 1, z, y] + r2[1]
                dh = dhs[s]
                xh = (xown[s].astype(F32) - st[s, :, 0:1]) * st[s, :, 1:2]
                ev = dh * gsrc[0:1, :]
                dgs[...] += jnp.sum((dh * xh).reshape(ROWS // 8, 8, DQ), axis=0)
                s1 = jnp.sum(ev, axis=1, keepdims=True)
                s2 = jnp.sum(ev * xh, axis=1, keepdims=True)
                lane = lax.broadcasted_iota(jnp.int32, (ROWS, 128), 1)
                mat = jnp.where(lane == 0, s1, jnp.where(lane == 1, s2, 0.0))
                pst[s] = mat.T[0:8, :]

    def h_load(s):
        return lc(hg.at[s], b1.at[s % 2], hld.at[s % 2])

    def u_load(s):
        return lc(ug.at[s], acc1.at[:, hcol(s % 2)], uld.at[s % 2])

    def q_store(s):
        return lc(acc1.at[:, hcol(s % 2)], ug.at[s], qst.at[s % 2])

    def p_store(s):
        return lc(acc3.at[:, hcol(s % 2)], vg.at[s], pstm.at[s % 2])

    def a_store(s):
        return lc(b0.at[s % 2, :, hcol(c)], ag.at[s, :, hcol(c)], ast.at[s % 2])

    def a_send(s):
        return rc(b0.at[s % 2, :, hcol(c)], ag.at[s, :, hcol(c)], cs.at[0, s], cr.at[0, s], CP)

    def a_load(s):
        return lc(ag.at[s, :, hcol(1 - c)], b0.at[s % 2, :, hcol(1 - c)], ald.at[0])

    def make_m(n):
        a_load(n).wait()
        rs_put(n, jnp.dot(b0[n % 2], w2o[...], preferred_element_type=F32))
        rs_first(n)

    h_load(0).start()
    u_load(0).start()
    dgs[...] = jnp.zeros_like(dgs)
    for k in range(3):
        wcopy(1, k).wait_recv()

    def pass2(K):
        s = K
        l1(1, s)

        @pl.when(K >= 2)
        def _():
            l2(1, K - 2)

        @pl.when(K >= 4)
        def _():
            l3(1, K - 4)

        @pl.when(K >= 1)
        def _():
            a_send(K - 1).wait_recv()
            a_load(K - 1).start()
            q_store(K - 1).wait()
        h_load(s).wait()
        u_load(s).wait()

        @pl.when(s < STEPS - 1)
        def _():
            h_load(s + 1).start()
            u_load(s + 1).start()

        @pl.when(s >= 2)
        def _():
            p_store(s - 2).wait()
            a_store(s - 2).wait()
            a_send(s - 2).wait_send()
        for k in range(2):
            cc = pl.ds(pl.multiple_of((s % 2) * FH + k * 512, 512), 512)
            v = jnp.dot(b1[s % 2], w3g[:, k * 512:(k + 1) * 512], preferred_element_type=F32)
            u = acc1[:, cc]
            sig = jax.nn.sigmoid(u)
            q = u * sig
            b0[s % 2, :, pl.ds(pl.multiple_of(c * FH + k * 512, 512), 512)] = (q * v).astype(BF16)
            acc3[:, cc] = v * sig * (1.0 + u * (1.0 - sig))
            acc1[:, cc] = q
        a_send(s).start()
        a_store(s).start()
        q_store(s).start()
        p_store(s).start()
        rs_loads(K)

        @pl.when(K >= 1)
        def _():
            make_m(K - 1)
        rs_proc(K)
    loop(STEPS, pass2)
    l2(1, STEPS - 2)
    l2(1, STEPS - 1)
    q_store(STEPS - 1).wait()
    for s in (STEPS - 2, STEPS - 1):
        p_store(s).wait()
        a_store(s).wait()

    def qp_loads(s):
        return [lc(ug.at[s], ub, dld.at[0]), lc(vg.at[s], vb, dld.at[1])]

    def d_send(w, s):
        src, dst = ((b0, dug), (b1, dvg))[w]
        return rc(src.at[s % 2, :, hcol(c)], dst.at[s], cs.at[1 + w, s], cr.at[1 + w, s], CP)

    def d_loads(s):
        return [lc(dug.at[s], b0.at[s % 2, :, hcol(1 - c)], ald.at[0]),
                lc(dvg.at[s], b1.at[s % 2, :, hcol(1 - c)], ald.at[1])]

    def w_loads(s):
        return [lc(ag.at[s], ab, ald.at[2]), lc(hg.at[s, :, qcol(tx)], hq, ald.at[3]), lc(dyg.at[tx, s], dyq, ald.at[4])]

    def next_loads(s):
        wait_block(1, s)
        for d in block_loads(1, s, dyb, xld) + qp_loads(s):
            d.start()

    a_send(STEPS - 1).wait_recv()
    a_load(STEPS - 1).start()
    for k in range(3):
        wcopy(2, k).wait_recv()
    next_loads(0)

    def st_copy(k, s):
        return rc(pst.at[s], pstr.at[k, s], ss.at[k, s], sr.at[k, s], (XP, XC, CP)[k])

    def pass3(i):
        K = i + 8
        s = i

        @pl.when(s < 4)
        def _():
            l3(1, s + 4)

        @pl.when((K >= 9) & (K <= 16))
        def _():
            d_send(0, K - 9).wait_recv()
            d_send(1, K - 9).wait_recv()
            for d in d_loads(K - 9) + w_loads(K - 9):
                d.start()

        @pl.when(s < STEPS)
        def _():
            for d in block_loads(1, s, dyb, xld) + qp_loads(s):
                d.wait()

            @pl.when(s < 2)
            def _():
                a_send(STEPS - 2 + s).wait_send()

            @pl.when(s >= 2)
            def _():
                d_send(0, s - 2).wait_send()
                d_send(1, s - 2).wait_send()
            for k in range(2):
                cc = pl.ds(pl.multiple_of(c * FH + k * 512, 512), 512)
                kk = slice(k * 512, (k + 1) * 512)
                da = lax.dot_general(dyb[...], w2g[kk, :], NT, preferred_element_type=F32)
                b0[s % 2, :, cc] = (da * vb[:, kk]).astype(BF16)
                b1[s % 2, :, cc] = (da * ub[:, kk]).astype(BF16)
            d_send(0, s).start()
            d_send(1, s).start()

            @pl.when(s < STEPS - 1)
            def _():
                next_loads(s + 1)
        rs_loads(K)

        @pl.when(K == 8)
        def _():
            make_m(STEPS - 1)
            for acc in (acc1, acc3, acc2):
                def zero(j):
                    acc[pl.ds(pl.multiple_of(j * 16, 16), 16), :] = jnp.zeros((16, FB), F32)
                loop(DQ // 16, zero)

        @pl.when((K >= 9) & (K <= 16))
        def _():
            n = K - 9
            for d in d_loads(n):
                d.wait()
            rs_put(8 + n, lax.dot_general(b0[n % 2], w1o[...], NT, preferred_element_type=F32)
                   + lax.dot_general(b1[n % 2], w3o[...], NT, preferred_element_type=F32))
            rs_first(8 + n)

        @pl.when(K >= 12)
        def _():
            for k in range(3):
                st_copy(k, K - 12).start()
        rs_proc(K)

        @pl.when((K >= 9) & (K <= 16))
        def _():
            n = K - 9
            for d in w_loads(n):
                d.wait()
            hqt[...] = hq[...].T
            dyqt[...] = dyq[...].T
            acc1[...] += jnp.dot(hqt[...], b0[n % 2], preferred_element_type=F32)
            acc3[...] += jnp.dot(hqt[...], b1[n % 2], preferred_element_type=F32)
            acc2[...] += jnp.dot(dyqt[...], ab[...], preferred_element_type=F32)

        @pl.when(K == 16)
        def _():
            for k, (acc, out) in enumerate(((acc1, dw1_ref), (acc3, dw3_ref), (acc2, dw2_ref))):
                lc(acc, out, wst.at[k]).start()
    loop(STEPS + 3, pass3)

    for k in range(3):
        st_copy(k, STEPS - 1).start()

    def dg_copy(k):
        return rc(dgs, dgr.at[k], dgss.at[k], dgsr.at[k], (YP, ZP, YZ)[k])
    for k in range(3):
        dg_copy(k).start()

    def dx_step(s):
        for k in range(3):
            st_copy(k, s).wait_recv()
        tot = pst[s] + pstr[0, s] + pstr[1, s] + pstr[2, s]
        mat = jnp.concatenate([tot, jnp.zeros((120, 128), F32)], axis=0).T
        m1 = mat[:, 0:1] * (1.0 / DM)
        m2 = mat[:, 1:2] * (1.0 / DM)
        inv = st[s, :, 1:2]
        xh = (xown[s].astype(F32) - st[s, :, 0:1]) * inv
        ev = dhs[s] * gsrc[0:1, :]
        dyown[s] = (dyown[s].astype(F32) + inv * (ev - m1 - xh * m2)).astype(BF16)
    loop(STEPS, dx_step)
    dx_out = lc(dyown, dx_ref, loc.at[0])
    dx_out.start()
    for k in range(3):
        dg_copy(k).wait_recv()
    tot = dgs[...] + dgr[0] + dgr[1] + dgr[2]
    dg_ref[...] = jnp.broadcast_to(jnp.sum(tot, axis=0, keepdims=True), (8, DQ))

    for k, (acc, out) in enumerate(((acc1, dw1_ref), (acc3, dw3_ref), (acc2, dw2_ref))):
        lc(acc, out, wst.at[k]).wait()
    y_store(STEPS - 2).wait()
    y_store(STEPS - 1).wait()
    for s in (STEPS - 2, STEPS - 1):
        d_send(0, s).wait_send()
        d_send(1, s).wait_send()

    def drain(s):
        for arr in range(2):
            for kind in range(9):
                gcopy(arr, kind, s).wait_send()
        for k in range(3):
            st_copy(k, s).wait_send()
    loop(STEPS, drain)
    for k in range(3):
        gaincopy(k).wait_send()
        dg_copy(k).wait_send()
        for w in range(3):
            wcopy(w, k).wait_send()
    dx_out.wait()


def solution(mesh):
    any_spec = pl.BlockSpec(memory_space=pl.ANY)
    vmem_spec = pl.BlockSpec(memory_space=pltpu.VMEM)
    sd = jax.ShapeDtypeStruct
    dma = pltpu.SemaphoreType.DMA

    def local_step(x_blk, dy_blk, gain_blk, w_gate_blk, w_up_blk, w_down_blk):
        outs = pl.pallas_call(
            kernel,
            out_shape=[
                sd((STEPS, ROWS, DQ), BF16), sd((STEPS, ROWS, DQ), BF16),
                sd((DQ, FB), F32), sd((DQ, FB), F32), sd((DQ, FB), F32), sd((8, DQ), F32),
                sd((4, STEPS, TOK, DQ), BF16), sd((4, STEPS, TOK, DQ), BF16),
                sd((STEPS, TOK, DM), BF16), sd((STEPS, TOK, FH), F32), sd((STEPS, TOK, FH), F32),
                sd((STEPS, TOK, FB), BF16), sd((STEPS, TOK, FH), BF16), sd((STEPS, TOK, FH), BF16),
                sd((2 * STEPS, 2, 2, ROWS, 256), F32), sd((2 * STEPS, 2, ROWS, 256), F32),
            ],
            in_specs=[any_spec, any_spec, vmem_spec, any_spec, any_spec, any_spec],
            out_specs=[any_spec] * 5 + [vmem_spec] + [any_spec] * 10,
            scratch_shapes=[
                pltpu.VMEM((DM, FH), BF16), pltpu.VMEM((DM, FH), BF16), pltpu.VMEM((FH, DM), BF16),
                pltpu.VMEM((DQ, FB), BF16), pltpu.VMEM((DQ, FB), BF16), pltpu.VMEM((FB, DQ), BF16),
                pltpu.VMEM((DQ, FB), F32), pltpu.VMEM((DQ, FB), F32), pltpu.VMEM((DQ, FB), F32),
                pltpu.VMEM((2, TOK, FB), BF16), pltpu.VMEM((2, TOK, FB), BF16),
                pltpu.VMEM((TOK, DM), BF16), pltpu.VMEM((TOK, FB), BF16),
                pltpu.VMEM((TOK, FH), F32), pltpu.VMEM((TOK, FH), F32),
                pltpu.VMEM((TOK, DQ), BF16), pltpu.VMEM((DQ, TOK), BF16),
                pltpu.VMEM((TOK, DQ), BF16), pltpu.VMEM((DQ, TOK), BF16),
                pltpu.VMEM((STEPS, ROWS, DQ), BF16), pltpu.VMEM((STEPS, ROWS, DQ), BF16),
                pltpu.VMEM((3, 2, 2, 2, ROWS, 256), F32),
                pltpu.VMEM((2, 2, ROWS, 256), F32), pltpu.VMEM((2, ROWS, 256), F32),
                pltpu.VMEM((8, DM), F32), pltpu.VMEM((8, DQ), F32),
                pltpu.VMEM((STEPS, ROWS, 128), F32), pltpu.VMEM((TOK, 128), F32),
                pltpu.VMEM((STEPS, ROWS, DQ), F32), pltpu.VMEM((2, ROWS, DQ), BF16),
                pltpu.VMEM((STEPS, 8, 128), F32), pltpu.VMEM((3, STEPS, 8, 128), F32),
                pltpu.VMEM((8, DQ), F32), pltpu.VMEM((3, 8, DQ), F32),
                dma((2, 9, STEPS)), dma((2, 9, STEPS)), dma((3, 3)), dma((3, 3)), dma((3,)), dma((3,)),
                dma((3, STEPS)), dma((3, STEPS)), dma((4, 2 * STEPS)), dma((4, 2 * STEPS)),
                dma((3, STEPS)), dma((3, STEPS)), dma((3,)), dma((3,)),
                dma((8,)), dma((1,)), dma((2,)), dma((2,)), dma((2,)), dma((2,)), dma((2,)), dma((2,)), dma((5,)),
                dma((2,)), dma((4,)), dma((2,)), dma((2,)), dma((3,)),
            ],
            compiler_params=pltpu.CompilerParams(collective_id=0, has_side_effects=True,
                                                 vmem_limit_bytes=67043328),
        )(x_blk.reshape(STEPS, ROWS, DQ), dy_blk.reshape(STEPS, ROWS, DQ), gain_blk.reshape(1, DQ),
          w_gate_blk, w_up_blk, w_down_blk)
        y_blk, dx_blk, dw1, dw3, dw2t, dg = outs[:6]
        return (y_blk.reshape(STEPS * ROWS, DQ), dx_blk.reshape(STEPS * ROWS, DQ), dw1, dw3, dw2t.T, dg[0])

    return jax.shard_map(
        local_step, mesh=mesh,
        in_specs=(P("ty", "tx"), P("ty", "tx"), P("tx"), P("tx", "ty"), P("tx", "ty"), P("ty", "tx")),
        out_specs=(P("ty", "tx"), P("ty", "tx"), P("tx", "ty"), P("tx", "ty"), P("ty", "tx"), P("tx")),
        check_vma=False)
```

time: 1340 us -> 361 us (0.27)
  waiting for transfers between devices: 1120 us -> 0 us
  Pallas kernels: 0 us -> 345 us
  matrix products: 143 us -> 0 us
  other arithmetic: 26.3 us -> 0 us
  blocking collectives: 24.6 us -> 0 us
  local copies, waits for them, and re-layouts: 1.25 us -> 15.6 us
  between operations: 14.9 us -> 0.65 us
    reduce_scatter x5 -> x0, waiting for transfers between devices: 769 us -> none  [the longest x1 230 us: local_step(): lax.psum_scatter(jnp.dot(h_all, w_gate_blk, preferred_element_type=jnp.fl...]
    all_gather x5 -> x0, waiting for transfers between devices: 347 us -> none  [the longest x1 103 us: local_step(): d_gate_all = lax.all_gather(d_gate, 'tx', axis=0, tiled=True)]
    pallas_call x0 -> x1, Pallas kernels: none -> 345 us  [local_step(): pl.pallas_call(kernel, out_shape=[sd((STEPS, ROWS, DQ), BF16), sd((STEPS,...]
    dot_general x9 -> x0, matrix products: 143 us -> none  [the longest x3 51.2 us: contract_cols(): lax.dot_general(left_op, right_op, (((1,), (1,)), ((), ())), preferred_el...]
    psum x3 -> x0, blocking collectives: 24.6 us -> none  [the longest x1 9.6 us: local_step(): d_gain_blk = lax.psum(jnp.sum(d_hnorm * x_hat, axis=0), 'ty')]
    convert_element_type x3 -> x0, other arithmetic: 22 us -> none  [the longest x1 15.3 us: local_step(): d_up = (d_act * gate_swish).astype(jnp.bfloat16)]
  transfers between devices with their start and end apart: 10 -> 0, of which waited for: 10 -> 0; matrix products, arithmetic and copies ran while one was open for 11% -> 0% of each run, Pallas kernels for 0% -> 0%
where the time goes in v2:
time: 361 us
  Pallas kernels  345 us (96%)
  local copies, waits for them, and re-layouts  15.6 us (4%)
    pallas_call x1, Pallas kernels, local_step(): pl.pallas_call(kernel, out_shape=[sd((STEPS, ROWS, DQ), BF16), sd((STEPS,...  345 us
    unnamed x11, local copies, waits for them, and re-layouts  14.3 us

profile of v2, /device:TPU:0, one launch (start us, length us, event | category | flops | bytes accessed | tf_op | source)
XLA Modules:
  0.0 361.0 jit_solution(2981449496894381906)
XLA Ops:
  0.6 344.7 %shard_map.109 = (bf16[8,128,512]{2,1,0:T(8,128)(2,1)}, bf16[8,128,512]{2,1,0:T(8,128)(2,1)}, f32[512,2048]{1,0:T(8,128)}, f32[512,2048]{1,0:T(8,128)}, f32[512,...) custom-call(bf16[8,128,512]{2,1,0:T(8,128)(2,1)} %bitcast.8, ...), custom_call_target="tpu_custom_call" | custom-call | tf_op jit(solution)/shard_map/pallas_call | solution.py:574
  345.4 1.3 slice.3
  346.7 0.0 copy-start.2
  346.7 0.0 copy-start.1
  346.7 5.5 %copy.12 = f32[2048,512]{1,0:T(8,128)} copy(f32[2048,512]{0,1:T(8,128)} %bitcast.7) | data formatting | bytes 8388608
  352.2 0.0 copy-done.2
  352.2 1.0 copy.17
  353.1 0.0 copy-done.1
  353.1 1.0 copy.18
  354.1 0.0 copy-start
  354.1 4.8 %copy.19 = f32[512,2048]{1,0:T(8,128)} copy(f32[512,2048]{1,0:T(8,128)} %get-tuple-element.32) | data formatting | bytes 8388608
  359.0 0.0 copy-done
  359.0 2.0 copy.20
Async XLA Ops:
  346.7 5.5 %copy-start.2 = (bf16[8,128,512]{2,1,0:T(8,128)(2,1)S(1)}, bf16[8,128,512]{2,1,0:T(8,128)(2,1)}, u32[]{:S(2)}) copy-start(bf16[8,128,512]{2,1,0:T(8,128)(2,1)} %get-tuple-element.12) | copy-start | bytes 3145732
  346.7 6.5 %copy-start.1 = (bf16[8,128,512]{2,1,0:T(8,128)(2,1)S(1)}, bf16[8,128,512]{2,1,0:T(8,128)(2,1)}, u32[]{:S(2)}) copy-start(bf16[8,128,512]{2,1,0:T(8,128)(2,1)} %get-tuple-element.13) | copy-start | bytes 3145732
  354.1 4.9 %copy-start = (f32[512,2048]{1,0:T(8,128)S(1)}, f32[512,2048]{1,0:T(8,128)}, u32[]{:S(2)}) copy-start(f32[512,2048]{1,0:T(8,128)} %get-tuple-element.33) | copy-start | bytes 12582916

commit v3 on v2

v3 whole, which is shorter than its diff:
```python
import jax
import jax.numpy as jnp
from jax import lax
from jax.experimental import pallas as pl
from jax.experimental.pallas import tpu as pltpu
from jax.sharding import PartitionSpec as P

LN_EPS = 1e-6
MESH = pl.DeviceIdType.MESH
BF16 = jnp.bfloat16
F32 = jnp.float32
STEPS = 8
ROWS = 128
TOK = 4 * ROWS
DQ = 512
DM = 4 * DQ
FB = 2048
FH = FB // 2
NT = (((1,), (1,)), ((), ()))
INV_DM = 1.0 / DM
PAIR, TRIO = range(2), range(3)
X, YA, YB, YBF, ZA, ZB, ZAF, C0, C1, YAF, XR = range(11)
RECV = [0, 1, 2, 2, 3, 4, 3, 5, 5, 1, 0]
DIRECT = 2
N_RS = 2 * STEPS
N_YAF = (STEPS - DIRECT) // 2


def alt(n):
    return n % 2


def kernel(x_ref, dy_ref, g_ref, wg_ref, wu_ref, wd_ref,
           y_ref, dx_ref, acc1, acc3, acc2, dg_ref,
           xg, dyg, hg, ug, vg,
           w1g, w3g, w2g, w2o, b0, b1, dyb, ub, vb,
           hq, hqt, xown, dyown, part, r1, r2, gfull, gsrc, st, stall, dhs,
           pst, pstr, dgs, dgr,
           gs, gr, ws, wr, ggs, ggr, cs, cr, rss, rsr, ss, sr, dgss, dgsr, loc, hst, ust, qst, pstm, hld, uld, ald,
           dld, xld, credit):
    ty = lax.axis_index("ty")
    tx = lax.axis_index("tx")
    y = ty % 2
    z = ty // 2
    c = tx % 2
    tx2 = (tx + 2) % 4
    ty_y = ty + 1 - 2 * y
    ty_z = (ty + 2) % 4
    XP = (ty, tx2)
    CP = (ty, tx + 1 - 2 * c)
    XC = (ty, tx2 + 1 - 2 * c)
    YP = (ty_y, tx)
    ZP = (ty_z, tx)
    YZ = (ty_z + 1 - 2 * y, tx)

    def rc(src, dst, s, r, dev):
        return pltpu.make_async_remote_copy(src_ref=src, dst_ref=dst, send_sem=s, recv_sem=r,
                                            device_id=dev, device_id_type=MESH)

    def lc(src, dst, s):
        return pltpu.make_async_copy(src, dst, s)

    def row(j):
        return pl.ds(pl.multiple_of(j * ROWS, ROWS), ROWS)

    def qcol(q):
        return pl.ds(pl.multiple_of(q * DQ, DQ), DQ)

    def hcol(h):
        return pl.ds(pl.multiple_of(h * FH, FH), FH)

    def gcopy(arr, kind, s):
        own, buf = ((x_ref, xg), (dy_ref, dyg))[arr]
        a, b = gs.at[arr, kind], gr.at[arr, RECV[kind], s]
        if kind in (X, YA, ZA):
            return rc(own.at[s], buf.at[tx, s, row(ty)], a, b, {X: XP, YA: YP, ZA: ZP}[kind])
        if kind in (YB, ZB):
            blk = buf.at[tx2, s, row(ty)]
            return rc(blk, blk, a, b, YP if kind == YB else ZP)
        if kind in (ZAF, YAF, YBF):
            blk = buf.at[tx2 if kind == YBF else tx, s, row(ty_y if kind == ZAF else ty_z)]
            return rc(blk, blk, a, b, ZP if kind == ZAF else YP)
        blk = buf.at[tx2 if kind == C1 else tx, s]
        return rc(blk, blk, a, b, XP if kind == XR else CP)

    def wait_bytes(ref, sem):
        lc(ref, ref, sem).wait()

    def pair_wait(arr, kind, s):
        wait_bytes(xg.at[0, s, 0:2 * ROWS], gr.at[arr, RECV[kind], s])

    def loop(n, f):
        def body(s, carry):
            f(s)
            return carry
        lax.fori_loop(0, n, body, 0)

    def wcopy(w, k):
        dev, h = ((XP, c), (XC, 1 - c), (CP, 1 - c))[k]
        a, b = ws.at[w, k], wr.at[w, k]
        if w < 2:
            return rc((wg_ref, wu_ref)[w].at[:, hcol(h)], (w1g, w3g)[w].at[qcol(tx), :], a, b, dev)
        return rc(wd_ref.at[hcol(h), :], w2g.at[:, qcol(tx)], a, b, dev)

    def gaincopy(k):
        return rc(gsrc, gfull.at[:, qcol(tx)], ggs.at[k], ggr.at[k], (XP, XC, CP)[k])

    gsrc[...] = jnp.broadcast_to(g_ref[...], (8, DQ))
    barrier = pltpu.get_barrier_semaphore()
    for dev in (XP, CP, XC, YP, ZP, YZ):
        pl.semaphore_signal(barrier, inc=1, device_id=dev, device_id_type=MESH)
    own_in = [lc(x_ref, xown, loc.at[0]), lc(dy_ref, dyown, loc.at[1])]
    w_in = [lc(wd_ref, w2o, loc.at[4]),
            lc(wg_ref.at[:, hcol(c)], w1g.at[qcol(tx), :], loc.at[5]),
            lc(wu_ref.at[:, hcol(c)], w3g.at[qcol(tx), :], loc.at[6]),
            lc(wd_ref.at[hcol(c), :], w2g.at[:, qcol(tx)], loc.at[7])]
    for d in own_in:
        d.start()
    with jax.named_scope("barrier"):
        pl.semaphore_wait(barrier, 6)

    for k in TRIO:
        gaincopy(k).start()
    loop(STEPS, lambda s: gcopy(0, X, s).start())

    def send_a(s):
        gcopy(0, YA, s).start()
        gcopy(0, ZA, s).start()
    loop(STEPS, send_a)
    for w in PAIR:
        for k in TRIO:
            wcopy(w, k).start()
    loop(DIRECT, lambda s: gcopy(1, X, s).start())
    for k in TRIO:
        wcopy(2, k).start()
    for d in w_in:
        d.start()
    for d in own_in:
        d.wait()
    own_out = [lc(xown, xg.at[tx, :, row(ty)], loc.at[0]), lc(dyown, dyg.at[tx, :, row(ty)], loc.at[1])]
    for d in own_out:
        d.start()
    gfull[:, qcol(tx)] = gsrc[...]

    def l1(arr, s):
        gcopy(arr, X, s).wait_recv()
        gcopy(arr, YB, s).start()
        gcopy(arr, ZB, s).start()

    def l1f(arr, s):
        gcopy(arr, YA, s).wait_recv()
        gcopy(arr, ZAF, s).start()

    def dy_forward(s):
        odd = (s >= DIRECT) & (alt(s) == 1)

        @pl.when(odd)
        def _():
            gcopy(1, ZA, s).wait_recv()
            gcopy(1, YAF, s).start()

        @pl.when(jnp.logical_not(odd))
        def _():
            gcopy(1, YA, s).wait_recv()
            gcopy(1, ZAF, s).start()

    def dy_quarter(s):
        odd = (s >= DIRECT) & (alt(s) == 1)

        @pl.when(odd)
        def _():
            pair_wait(1, YA, s)

        @pl.when(jnp.logical_not(odd))
        def _():
            pair_wait(1, ZA, s)
        gcopy(1, C0, s).start()

        @pl.when(s >= DIRECT)
        def _():
            gcopy(1, XR, s).start()

    def dy_rest(s):
        pair_wait(1, YB, s)
        gcopy(1, C1, s).start()

    def dy_cross(s):
        gcopy(1, XR, s).wait_recv()
        gcopy(1, C1, s).start()

    def l2(arr, s):
        gcopy(arr, ZB, s).wait_recv()
        gcopy(arr, YBF, s).start()

    def l3(arr, s):
        pair_wait(arr, ZA, s)
        gcopy(arr, C0, s).start()
        pair_wait(arr, YB, s)
        gcopy(arr, C1, s).start()

    def first(s):
        l1(0, s)
        l1f(0, s)
    with jax.named_scope("g_first"):
        loop(STEPS, first)
    with jax.named_scope("g_l2"):
        loop(STEPS, lambda s: l2(0, s))

    def send_dya(s):
        gcopy(1, YA, s).start()
        gcopy(1, ZA, s).start()
    loop(STEPS, send_dya)
    with jax.named_scope("g_local"):
        for d in own_out:
            d.wait()
        for d in w_in:
            d.wait()
        for k in TRIO:
            gaincopy(k).wait_recv()
    with jax.named_scope("g_l3"):
        loop(STEPS, lambda s: l3(0, s))

    def block_loads(arr, s, dst, sem):
        buf = (xg, dyg)[arr]
        return [lc(buf.at[q, s], dst.at[:, q * DQ:(q + 1) * DQ], sem.at[q]) for q in range(4)]

    def wait_block(arr, s):
        wait_bytes(xg.at[0:2, s], gr.at[arr, RECV[C0], s])

    xs, hb = b1.at[0], b1.at[1]

    def h_store(s):
        return lc(hb, hg.at[s], hst.at[0])

    def u_store(s):
        return lc(acc2.at[:, hcol(alt(s))], ug.at[s], ust.at[alt(s)])

    wait_block(0, 0)
    for d in block_loads(0, 0, xs, xld):
        d.start()
    with jax.named_scope("w1_wait"):
        for k in TRIO:
            wcopy(0, k).wait_recv()

    def pass1(s):
        with jax.named_scope("p1_xwait"):
            for d in block_loads(0, s, xs, xld):
                d.wait()

        @pl.when(s >= 1)
        def _():
            h_store(s - 1).wait()

        def chunk(i):
            rr = pl.ds(pl.multiple_of(i * 64, 64), 64)
            xf = xs[rr, :].astype(F32)
            mu = jnp.sum(xf, axis=1, keepdims=True) * INV_DM
            sq = jnp.sum(xf * xf, axis=1, keepdims=True) * INV_DM
            inv = lax.rsqrt(sq - mu * mu + LN_EPS)
            hb[rr, :] = (gfull[0:1, :] * ((xf - mu) * inv)).astype(BF16)
            lane = lax.broadcasted_iota(jnp.int32, (64, 128), 1)
            stall[rr, :] = jnp.where(lane == 0, mu, inv)
        with jax.named_scope("p1_ln"):
            loop(TOK // 64, chunk)
        st[s] = stall[row(ty), :]
        h_store(s).start()

        @pl.when(s < STEPS - 1)
        def _():
            wait_block(0, s + 1)
            for d in block_loads(0, s + 1, xs, xld):
                d.start()

        @pl.when(s >= 2)
        def _():
            u_store(s - 2).wait()
        with jax.named_scope("p1_dot"):
            acc2[:, hcol(alt(s))] = jnp.dot(hb[...], w1g[...], preferred_element_type=F32)
        u_store(s).start()
        with jax.named_scope("p1_fwd"):
            dy_forward(s)
    loop(STEPS, pass1)
    h_store(STEPS - 1).wait()
    u_store(STEPS - 2).wait()
    u_store(STEPS - 1).wait()

    def rs_copy(kind, n):
        slot = n % 3
        a, b = rss.at[kind, n % 4], rsr.at[kind, n % 4]
        if kind == 0:
            return rc(part.at[slot, 0, 1 - y], r1.at[n % 3, 0], a, b, YP)
        if kind == 1:
            return rc(part.at[slot, 1, 1 - z], r1.at[n % 3, 1], a, b, ZP)
        if kind == 2:
            return rc(part.at[slot, 0, y, 1 - z], r2.at[n % 3, 0], a, b, ZP)
        return rc(part.at[slot, 1, z, 1 - y], r2.at[n % 3, 1], a, b, YP)

    def rs_put(n, val):
        slot = n % 3
        for j in range(4):
            part[slot, 0, j % 2, j // 2] = val[j * ROWS:(j + 1) * ROWS, 0:256]
            part[slot, 1, j // 2, j % 2] = val[j * ROWS:(j + 1) * ROWS, 256:512]

    def rs_first(n):
        rs_copy(0, n).start()
        rs_copy(1, n).start()

    def rs_proc(K):
        @pl.when((K >= 2) & (K < N_RS + 2))
        def _():
            n = K - 2
            slot = n % 3
            for k in PAIR:
                rs_copy(k, n).wait_recv()
            for k in PAIR:
                part[slot, 0, y, k] += r1[slot, 0, k]
                part[slot, 1, z, k] += r1[slot, 1, k]
            rs_copy(2, n).start()
            rs_copy(3, n).start()

        @pl.when(K >= 3)
        def _():
            n = K - 3
            slot = n % 3
            for k in PAIR:
                rs_copy(2 + k, n).wait_recv()
            m0, m1 = r2[slot, 0], r2[slot, 1]
            for k in range(4):
                rs_copy(k, n).wait_send()

            @pl.when(n < 8)
            def _():
                y_ref[n, :, 0:256] = (xown[n, :, 0:256].astype(F32) + (part[slot, 0, y, z] + m0)).astype(BF16)
                y_ref[n, :, 256:512] = (xown[n, :, 256:512].astype(F32) + (part[slot, 1, z, y] + m1)).astype(BF16)

            @pl.when(n >= 8)
            def _():
                s = n - 8
                dhs[s % 4, :, 0:256] = part[slot, 0, y, z] + m0
                dhs[s % 4, :, 256:512] = part[slot, 1, z, y] + m1
                dh = dhs[s % 4]
                xh = (xown[s].astype(F32) - st[s, :, 0:1]) * st[s, :, 1:2]
                ev = dh * gsrc[0:1, :]
                dgs[...] += jnp.sum((dh * xh).reshape(ROWS // 8, 8, DQ), axis=0)
                s1 = jnp.sum(ev, axis=1, keepdims=True)
                s2 = jnp.sum(ev * xh, axis=1, keepdims=True)
                lane = lax.broadcasted_iota(jnp.int32, (ROWS, 128), 1)
                mat = jnp.where(lane == 0, s1, jnp.where(lane == 1, s2, 0.0))
                pst[s] = mat.T[0:8, :]

    def h_load(s):
        return lc(hg.at[s], b1.at[alt(s)], hld.at[alt(s)])

    def u_load(s):
        return lc(ug.at[s], acc1.at[:, hcol(alt(s))], uld.at[alt(s)])

    def q_store(s):
        return lc(acc1.at[:, hcol(alt(s))], ug.at[s], qst.at[alt(s)])

    def p_store(s):
        return lc(acc3.at[:, hcol(alt(s))], vg.at[s], pstm.at[alt(s)])

    def quart(k):
        return pl.ds(pl.multiple_of(c * FH + k * DQ, DQ), DQ)

    def swap(buf, s, k):
        blk = (b0, b1)[buf].at[alt(s), :, quart(k)]
        return rc(blk, blk, cs.at[buf, alt(s), k], cr.at[buf, alt(s), k], CP)

    def slot_free():
        pl.semaphore_signal(credit, inc=1, device_id=CP, device_id_type=MESH)

    def slot_wait():
        pl.semaphore_wait(credit, 1)

    def dyq_load(s):
        return lc(dyg.at[tx, s], hq, ald.at[1])

    def make_m(n):
        for k in PAIR:
            swap(0, n, k).wait_recv()
        rs_put(n, jnp.dot(b0[alt(n)], w2o[...], preferred_element_type=F32))
        rs_first(n)

    def add_dw2(n):
        dyq_load(n).wait()
        hqt[...] = hq[...].T
        acc2[...] += jnp.dot(hqt[...], b0[alt(n)], preferred_element_type=F32)
        slot_free()

    def zero(acc):
        def body(j):
            acc[pl.ds(pl.multiple_of(j * 16, 16), 16), :] = jnp.zeros((16, FB), F32)
        loop(DQ // 16, body)

    def qp_loads(s):
        return [lc(ug.at[s], ub, dld.at[0]), lc(vg.at[s], vb, dld.at[1])]

    def w_load(s):
        return lc(hg.at[s, :, qcol(tx)], hq, ald.at[0])

    def next_loads(s):
        wait_block(1, s)
        for d in block_loads(1, s, dyb, xld) + qp_loads(s):
            d.start()

    zero(acc2)
    h_load(0).start()
    u_load(0).start()
    dgs[...] = jnp.zeros_like(dgs)
    with jax.named_scope("w3_wait"):
        for k in TRIO:
            wcopy(1, k).wait_recv()

    own_w = [lc(w.at[:, hcol(h)], w1g.at[qcol(2 * k + h), :], loc.at[2 * k + h])
             for k, w in enumerate((wg_ref, wu_ref)) for h in PAIR]
    for d in own_w:
        d.start()

    def pass2(K):
        s = K
        with jax.named_scope("p2_comm"):
            dy_quarter(K)

            @pl.when((K >= 1) & (K <= DIRECT))
            def _():
                l1(1, K - 1)

            @pl.when((K >= 3) & (K <= 2 + DIRECT))
            def _():
                l2(1, K - 3)

            @pl.when((K >= 5) & (K <= 4 + DIRECT))
            def _():
                dy_rest(K - 5)

        @pl.when(K >= 1)
        def _():
            with jax.named_scope("p2_m"):
                make_m(K - 1)
                q_store(K - 1).wait()
        with jax.named_scope("p2_huwait"):
            h_load(s).wait()
            u_load(s).wait()

        @pl.when(s < STEPS - 1)
        def _():
            h_load(s + 1).start()
            u_load(s + 1).start()

        @pl.when(s == STEPS - 1)
        def _():
            next_loads(0)

        @pl.when(s >= 2)
        def _():
            p_store(s - 2).wait()
            for k in PAIR:
                swap(0, s - 2, k).wait_send()
            slot_wait()
        with jax.named_scope("p2_dot"):
            for k in PAIR:
                cc = pl.ds(pl.multiple_of((alt(s)) * FH + k * DQ, DQ), DQ)
                v = jnp.dot(b1[alt(s)], w3g[:, k * DQ:(k + 1) * DQ], preferred_element_type=F32)
                u = acc1[:, cc]
                sig = jax.nn.sigmoid(u)
                q = u * sig
                b0[alt(s), :, quart(k)] = (q * v).astype(BF16)
                acc3[:, cc] = v * sig * (1.0 + u * (1.0 - sig))
                acc1[:, cc] = q
                if k:
                    swap(0, s, 0).start()
        swap(0, s, 1).start()
        q_store(s).start()
        p_store(s).start()
        @pl.when(K >= 1)
        def _():
            with jax.named_scope("p2_dw2"):
                add_dw2(K - 1)
        dyq_load(s).start()
        with jax.named_scope("p2_rsp"):
            rs_proc(K)
    loop(STEPS, pass2)
    for d in own_w:
        d.wait()
    q_store(STEPS - 1).wait()
    for s in (STEPS - 2, STEPS - 1):
        p_store(s).wait()

    with jax.named_scope("w2_wait"):
        for k in TRIO:
            wcopy(2, k).wait_recv()

    def st_copy(k, s):
        return rc(pst.at[s], pstr.at[k, s], ss.at[k], sr.at[k, s], (XP, XC, CP)[k])

    def dx_step(s):
        for k in TRIO:
            st_copy(k, s).wait_recv()
        tot = pst[s] + pstr[0, s] + pstr[1, s] + pstr[2, s]
        mat = jnp.concatenate([tot, jnp.zeros((120, 128), F32)], axis=0).T
        m1 = mat[:, 0:1] * INV_DM
        m2 = mat[:, 1:2] * INV_DM
        inv = st[s, :, 1:2]
        xh = (xown[s].astype(F32) - st[s, :, 0:1]) * inv
        ev = dhs[s % 4] * gsrc[0:1, :]
        dx_ref[s] = (dyown[s].astype(F32) + inv * (ev - m1 - xh * m2)).astype(BF16)

    def pass3(i):
        K = i + STEPS
        s = i
        n = i - 1
        busy = (n >= 0) & (n < STEPS)

        @pl.when(s == 0)
        def _():
            make_m(STEPS - 1)

        @pl.when(busy)
        def _():
            with jax.named_scope("p3_dload"):
                for w in PAIR:
                    for k in PAIR:
                        swap(w, n, k).wait_recv()
            with jax.named_scope("p3_dh"):
                dh = jnp.zeros((TOK, DQ), F32)
                for j in range(4):
                    left = (b0, b1)[j // 2][alt(n), :, (j % 2) * FH:(j % 2 + 1) * FH]
                    dh = dh + lax.dot_general(left, w1g[j * DQ:(j + 1) * DQ, :], NT, preferred_element_type=F32)
                rs_put(STEPS + n, dh)
            rs_first(STEPS + n)

        @pl.when(s < STEPS)
        def _():
            with jax.named_scope("p3_ldwait"):
                for d in block_loads(1, s, dyb, xld) + qp_loads(s):
                    d.wait()

            for k in PAIR:
                swap(0, s, k).wait_send()

            @pl.when(s >= 2)
            def _():
                for k in PAIR:
                    swap(1, s, k).wait_send()
            slot_wait()
            with jax.named_scope("p3_da"):
                for k in PAIR:
                    cc = quart(k)
                    kk = slice(k * DQ, (k + 1) * DQ)
                    da = lax.dot_general(dyb[...], w2g[kk, :], NT, preferred_element_type=F32)
                    b0[alt(s), :, cc] = (da * vb[:, kk]).astype(BF16)
                    b1[alt(s), :, cc] = (da * ub[:, kk]).astype(BF16)
                    if k:
                        swap(0, s, 0).start()
                        swap(1, s, 0).start()
            swap(0, s, 1).start()
            swap(1, s, 1).start()

            @pl.when(s < STEPS - 1)
            def _():
                with jax.named_scope("p3_nextl"):
                    next_loads(s + 1)
        @pl.when(s == 0)
        def _():
            add_dw2(STEPS - 1)
            zero(acc1)
            zero(acc3)

        @pl.when(busy)
        def _():
            w_load(n).wait()
            with jax.named_scope("p3_dw"):
                hqt[...] = hq[...].T
                acc1[...] += jnp.dot(hqt[...], b0[alt(n)], preferred_element_type=F32)
                acc3[...] += jnp.dot(hqt[...], b1[alt(n)], preferred_element_type=F32)

            @pl.when(n < STEPS - 2)
            def _():
                slot_free()

        @pl.when(s < STEPS)
        def _():
            w_load(s).start()

        @pl.when(s < STEPS - DIRECT)
        def _():
            with jax.named_scope("p3_cross"):
                dy_cross(s + DIRECT)

        @pl.when(s >= 4)
        def _():
            for k in TRIO:
                st_copy(k, s - 4).start()

        @pl.when(s >= 5)
        def _():
            with jax.named_scope("p3_dx"):
                dx_step(s - 5)
        with jax.named_scope("p3_rsp"):
            rs_proc(K)
    loop(STEPS + 3, pass3)

    for k in TRIO:
        st_copy(k, STEPS - 1).start()

    def dg_copy(k):
        return rc(dgs, dgr.at[k], dgss.at[k], dgsr.at[k], (YP, ZP, YZ)[k])
    for k in TRIO:
        dg_copy(k).start()

    with jax.named_scope("t_dx"):
        for s in (STEPS - 2, STEPS - 1):
            dx_step(s)
    with jax.named_scope("t_dg"):
        for k in TRIO:
            dg_copy(k).wait_recv()
    tot = dgs[...] + dgr[0] + dgr[1] + dgr[2]
    dg_ref[...] = jnp.broadcast_to(jnp.sum(tot, axis=0, keepdims=True), (8, DQ))

    with jax.named_scope("t_out"):
        for s in (STEPS - 2, STEPS - 1):
            for w in PAIR:
                for k in PAIR:
                    swap(w, s, k).wait_send()
    with jax.named_scope("t_drain"):
        for kind in (X, YA, YB, YBF, ZA, ZB, ZAF):
            wait_bytes(xown, gs.at[0, kind])
        for arr in PAIR:
            for kind in (C0, C1):
                wait_bytes(xg.at[0], gs.at[arr, kind])
        for kind in (YA, ZA):
            wait_bytes(xown, gs.at[1, kind])
        for kind in (X, YB, YBF, ZB):
            wait_bytes(xown.at[0:DIRECT], gs.at[1, kind])
        wait_bytes(xown.at[0:N_YAF], gs.at[1, YAF])
        wait_bytes(xown.at[N_YAF:], gs.at[1, ZAF])
        wait_bytes(xg.at[0, DIRECT:], gs.at[1, XR])
        for k in TRIO:
            wait_bytes(pst, ss.at[k])
            gaincopy(k).wait_send()
            dg_copy(k).wait_send()
            for w in TRIO:
                wcopy(w, k).wait_send()


def finish(y_in, dx_in, dw1_in, dw3_in, dw2_in, dg_in, y_ref, dx_ref, dw1_ref, dw3_ref, dw2_ref, dg_ref, dw2_out, sem):
    outs = [pltpu.make_async_copy(src, dst, sem.at[k]) for k, (src, dst) in enumerate(
        ((dw1_in, dw1_ref), (dw3_in, dw3_ref), (y_in, y_ref), (dx_in, dx_ref)))]
    for d in outs:
        d.start()
    dg_ref[...] = dg_in[0:1, :]
    for i in range(4):
        cols = slice(i * DQ, (i + 1) * DQ)
        dw2_out[cols, :] = dw2_in[:, cols].T
        d = pltpu.make_async_copy(dw2_out.at[cols, :], dw2_ref.at[cols, :], sem.at[4 + i])
        d.start()
        outs.append(d)
    for d in outs:
        d.wait()


def solution(mesh):
    any_spec = pl.BlockSpec(memory_space=pl.ANY)
    vmem_spec = pl.BlockSpec(memory_space=pltpu.VMEM)
    sd = jax.ShapeDtypeStruct
    vm = pltpu.VMEM
    dma = pltpu.SemaphoreType.DMA
    d2, d3 = dma((2,)), dma((3,))

    def local_step(x_blk, dy_blk, gain_blk, w_gate_blk, w_up_blk, w_down_blk):
        outs = pl.pallas_call(
            kernel,
            out_shape=[
                vm((STEPS, ROWS, DQ), BF16), vm((STEPS, ROWS, DQ), BF16),
                vm((DQ, FB), F32), vm((DQ, FB), F32), vm((DQ, FB), F32), vm((8, DQ), F32),
                sd((4, STEPS, TOK, DQ), BF16), sd((4, STEPS, TOK, DQ), BF16),
                sd((STEPS, TOK, DM), BF16), sd((STEPS, TOK, FH), F32), sd((STEPS, TOK, FH), F32),
            ],
            in_specs=[any_spec, any_spec, vmem_spec, any_spec, any_spec, any_spec],
            out_specs=[vmem_spec] * 6 + [any_spec] * 5,
            scratch_shapes=[
                pltpu.VMEM((DM, FH), BF16), pltpu.VMEM((DM, FH), BF16), pltpu.VMEM((FH, DM), BF16),
                pltpu.VMEM((FB, DQ), BF16),
                pltpu.VMEM((2, TOK, FB), BF16), pltpu.VMEM((2, TOK, FB), BF16),
                pltpu.VMEM((TOK, DM), BF16),
                pltpu.VMEM((TOK, FH), F32), pltpu.VMEM((TOK, FH), F32),
                pltpu.VMEM((TOK, DQ), BF16), pltpu.VMEM((DQ, TOK), BF16),
                pltpu.VMEM((STEPS, ROWS, DQ), BF16), pltpu.VMEM((STEPS, ROWS, DQ), BF16),
                pltpu.VMEM((3, 2, 2, 2, ROWS, 256), F32),
                pltpu.VMEM((3, 2, 2, ROWS, 256), F32), pltpu.VMEM((3, 2, ROWS, 256), F32),
                pltpu.VMEM((8, DM), F32), pltpu.VMEM((8, DQ), F32),
                pltpu.VMEM((STEPS, ROWS, 128), F32), pltpu.VMEM((TOK, 128), F32),
                pltpu.VMEM((4, ROWS, DQ), F32),
                pltpu.VMEM((STEPS, 8, 128), F32), pltpu.VMEM((3, STEPS, 8, 128), F32),
                pltpu.VMEM((8, DQ), F32), pltpu.VMEM((3, 8, DQ), F32),
                dma((2, 11)), dma((2, 6, STEPS)), dma((3, 3)), dma((3, 3)), d3, d3,
                dma((2, 2, 2)), dma((2, 2, 2)), dma((4, 4)), dma((4, 4)),
                d3, dma((3, STEPS)), d3, d3,
                dma((8,)), dma((1,)), d2, d2, d2, d2, d2, d2,
                d2, dma((4,)), pltpu.SemaphoreType.REGULAR,
            ],
            compiler_params=pltpu.CompilerParams(collective_id=0, has_side_effects=True,
                                                 vmem_limit_bytes=67043328 - 14 * 2**20 - 2**16),
        )(x_blk.reshape(STEPS, ROWS, DQ), dy_blk.reshape(STEPS, ROWS, DQ), gain_blk.reshape(1, DQ),
          w_gate_blk, w_up_blk, w_down_blk)
        y_blk, dx_blk, dw1, dw3, dw2, dg = pl.pallas_call(
            finish,
            out_shape=[sd((STEPS, ROWS, DQ), BF16), sd((STEPS, ROWS, DQ), BF16), sd((DQ, FB), F32), sd((DQ, FB), F32),
                       sd((FB, DQ), F32), sd((1, DQ), F32)],
            in_specs=[vmem_spec] * 6,
            out_specs=[any_spec] * 5 + [vmem_spec],
            scratch_shapes=[pltpu.VMEM((FB, DQ), F32), dma((8,))],
            compiler_params=pltpu.CompilerParams(vmem_limit_bytes=20 * 2**20),
        )(*outs[:6])
        return (y_blk.reshape(STEPS * ROWS, DQ), dx_blk.reshape(STEPS * ROWS, DQ), dw1, dw3, dw2, dg.reshape(DQ))

    return jax.shard_map(
        local_step, mesh=mesh,
        in_specs=(P("ty", "tx"), P("ty", "tx"), P("tx"), P("tx", "ty"), P("tx", "ty"), P("ty", "tx")),
        out_specs=(P("ty", "tx"), P("ty", "tx"), P("tx", "ty"), P("tx", "ty"), P("ty", "tx"), P("tx")),
        check_vma=False)
```

time: 361 us -> 284 us (0.79)
  Pallas kernels: 345 us -> 283 us
  local copies, waits for them, and re-layouts: 15.6 us -> 0 us
    pallas_call x1 -> x2, Pallas kernels: 345 us -> 283 us  [the longest x1 277 us: local_step(): pl.pallas_call(kernel, out_shape=[vm((STEPS, ROWS, DQ), BF16), vm((STEPS,...]
    unnamed x11 -> x0, local copies, waits for them, and re-layouts: 14.3 us -> none
where the time goes in v3:
time: 284 us
  Pallas kernels  283 us (100%)
    pallas_call x1, Pallas kernels, local_step(): pl.pallas_call(kernel, out_shape=[vm((STEPS, ROWS, DQ), BF16), vm((STEPS,...  277 us
    pallas_call x1, Pallas kernels, local_step(): pl.pallas_call(finish, out_shape=[sd((STEPS, ROWS, DQ), BF16), sd((STEPS,...  5.85 us

profile of v3, /device:TPU:0, one launch (start us, length us, event | category | flops | bytes accessed | tf_op | source)
XLA Modules:
  0.0 283.8 jit_solution(5541507983702696585)
XLA Ops:
  0.6 277.1 %shard_map.109 = (bf16[8,128,512]{2,1,0:T(8,128)(2,1)S(1)}, bf16[8,128,512]{2,1,0:T(8,128)(2,1)S(1)}, f32[512,2048]{1,0:T(8,128)S(1)}, f32[512,2048]{1,0:T(8,128...) custom-call(bf16[8,128,512]{2,1,0:T(8,128)(2,1)} %bitcast.6, ...), custom_call_target="tpu_custom_call" | custom-call | tf_op jit(solution)/shard_map/pallas_call | solution.py:672
  277.8 5.9 %shard_map.110 = (bf16[8,128,512]{2,1,0:T(8,128)(2,1)}, bf16[8,128,512]{2,1,0:T(8,128)(2,1)}, f32[512,2048]{1,0:T(8,128)}, f32[512,2048]{1,0:T(8,128)}, f32[2048,512]{1,0:T(8,128)}, /*index=5*/f32[1,512]{1,0:T(1,128)}) custom-call(bf16[8,128,512]{2,1,0:T(8,128)(2,1)S(1)} %get-tuple-element.18.y_in, bf16[8,128,512]{2,1,0:T(8,128)(2,1)S(1)} %get-tuple-element.19.dx_in, ...), custom_call_target="tpu_custom_call" | custom-call | tf_op jit(solution)/shard_map/pallas_call | solution.py:707

commit v4 on v3

--- a/solution.py
+++ b/solution.py
@@ -19,11 +19,13 @@
 NT = (((1,), (1,)), ((), ()))
 INV_DM = 1.0 / DM
 PAIR, TRIO = range(2), range(3)
-X, YA, YB, YBF, ZA, ZB, ZAF, C0, C1, YAF, XR = range(11)
-RECV = [0, 1, 2, 2, 3, 4, 3, 5, 5, 1, 0]
+X, YA, YB, YBF, ZA, ZB, ZAF, C0, C1, YAF, XR, ZBF = range(12)
+RECV = [0, 1, 2, 2, 3, 4, 3, 5, 5, 1, 0, 4]
 DIRECT = 2
+DX_LAG = 6
+DX_SLOTS = DX_LAG - 2
 N_RS = 2 * STEPS
-N_YAF = (STEPS - DIRECT) // 2
+N_YAF = (STEPS - DIRECT + 1) // 2
 
 
 def alt(n):
@@ -77,9 +79,10 @@
         if kind in (YB, ZB):
             blk = buf.at[tx2, s, row(ty)]
             return rc(blk, blk, a, b, YP if kind == YB else ZP)
-        if kind in (ZAF, YAF, YBF):
-            blk = buf.at[tx2 if kind == YBF else tx, s, row(ty_y if kind == ZAF else ty_z)]
-            return rc(blk, blk, a, b, ZP if kind == ZAF else YP)
+        if kind in (ZAF, YAF, YBF, ZBF):
+            to_z = kind in (ZAF, ZBF)
+            blk = buf.at[tx2 if kind in (YBF, ZBF) else tx, s, row(ty_y if to_z else ty_z)]
+            return rc(blk, blk, a, b, ZP if to_z else YP)
         blk = buf.at[tx2 if kind == C1 else tx, s]
         return rc(blk, blk, a, b, XP if kind == XR else CP)
 
@@ -180,8 +183,24 @@
         def _():
             gcopy(1, XR, s).start()
 
+    def dy_l2(s):
+        @pl.when(s == 1)
+        def _():
+            gcopy(1, YB, s).wait_recv()
+            gcopy(1, ZBF, s).start()
+
+        @pl.when(s != 1)
+        def _():
+            l2(1, s)
+
     def dy_rest(s):
-        pair_wait(1, YB, s)
+        @pl.when(s == 1)
+        def _():
+            pair_wait(1, ZB, s)
+
+        @pl.when(s != 1)
+        def _():
+            pair_wait(1, YB, s)
         gcopy(1, C1, s).start()
 
     def dy_cross(s):
@@ -336,9 +355,9 @@
             @pl.when(n >= 8)
             def _():
                 s = n - 8
-                dhs[s % 4, :, 0:256] = part[slot, 0, y, z] + m0
-                dhs[s % 4, :, 256:512] = part[slot, 1, z, y] + m1
-                dh = dhs[s % 4]
+                dhs[s % DX_SLOTS, :, 0:256] = part[slot, 0, y, z] + m0
+                dhs[s % DX_SLOTS, :, 256:512] = part[slot, 1, z, y] + m1
+                dh = dhs[s % DX_SLOTS]
                 xh = (xown[s].astype(F32) - st[s, :, 0:1]) * st[s, :, 1:2]
                 ev = dh * gsrc[0:1, :]
                 dgs[...] += jnp.sum((dh * xh).reshape(ROWS // 8, 8, DQ), axis=0)
@@ -408,9 +427,14 @@
     h_load(0).start()
     u_load(0).start()
     dgs[...] = jnp.zeros_like(dgs)
+    last = tx2 + 1 - 2 * c
+    for k in (2, 0):
+        wcopy(1, k).wait_recv()
+    h_load(0).wait()
+    acc3[:, 0:FH] = sum(jnp.dot(b1[0, :, qcol(q)], w3g[qcol(q), :], preferred_element_type=F32)
+                        for q in (tx, tx + 1 - 2 * c, tx2))
     with jax.named_scope("w3_wait"):
-        for k in TRIO:
-            wcopy(1, k).wait_recv()
+        wcopy(1, 1).wait_recv()
 
     own_w = [lc(w.at[:, hcol(h)], w1g.at[qcol(2 * k + h), :], loc.at[2 * k + h])
              for k, w in enumerate((wg_ref, wu_ref)) for h in PAIR]
@@ -428,7 +452,7 @@
 
             @pl.when((K >= 3) & (K <= 2 + DIRECT))
             def _():
-                l2(1, K - 3)
+                dy_l2(K - 3)
 
             @pl.when((K >= 5) & (K <= 4 + DIRECT))
             def _():
@@ -440,7 +464,9 @@
                 make_m(K - 1)
                 q_store(K - 1).wait()
         with jax.named_scope("p2_huwait"):
-            h_load(s).wait()
+            @pl.when(s > 0)
+            def _():
+                h_load(s).wait()
             u_load(s).wait()
 
         @pl.when(s < STEPS - 1)
@@ -458,18 +484,29 @@
             for k in PAIR:
                 swap(0, s - 2, k).wait_send()
             slot_wait()
-        with jax.named_scope("p2_dot"):
-            for k in PAIR:
-                cc = pl.ds(pl.multiple_of((alt(s)) * FH + k * DQ, DQ), DQ)
-                v = jnp.dot(b1[alt(s)], w3g[:, k * DQ:(k + 1) * DQ], preferred_element_type=F32)
-                u = acc1[:, cc]
-                sig = jax.nn.sigmoid(u)
-                q = u * sig
-                b0[alt(s), :, quart(k)] = (q * v).astype(BF16)
-                acc3[:, cc] = v * sig * (1.0 + u * (1.0 - sig))
-                acc1[:, cc] = q
-                if k:
-                    swap(0, s, 0).start()
+        def gate(k, v):
+            cc = pl.ds(pl.multiple_of(alt(s) * FH + k * DQ, DQ), DQ)
+            u = acc1[:, cc]
+            sig = jax.nn.sigmoid(u)
+            q = u * sig
+            b0[alt(s), :, quart(k)] = (q * v).astype(BF16)
+            acc3[:, cc] = v * sig * (1.0 + u * (1.0 - sig))
+            acc1[:, cc] = q
+            if k:
+                swap(0, s, 0).start()
+
+        @pl.when(s > 0)
+        def _():
+            with jax.named_scope("p2_dot"):
+                for k in PAIR:
+                    gate(k, jnp.dot(b1[alt(s)], w3g[:, k * DQ:(k + 1) * DQ], preferred_element_type=F32))
+
+        @pl.when(s == 0)
+        def _():
+            with jax.named_scope("p2_dot0"):
+                for k in PAIR:
+                    kk = slice(k * DQ, (k + 1) * DQ)
+                    gate(k, acc3[:, kk] + jnp.dot(b1[0, :, qcol(last)], w3g[qcol(last), kk], preferred_element_type=F32))
         swap(0, s, 1).start()
         q_store(s).start()
         p_store(s).start()
@@ -503,7 +540,7 @@
         m2 = mat[:, 1:2] * INV_DM
         inv = st[s, :, 1:2]
         xh = (xown[s].astype(F32) - st[s, :, 0:1]) * inv
-        ev = dhs[s % 4] * gsrc[0:1, :]
+        ev = dhs[s % DX_SLOTS] * gsrc[0:1, :]
         dx_ref[s] = (dyown[s].astype(F32) + inv * (ev - m1 - xh * m2)).astype(BF16)
 
     def pass3(i):
@@ -529,6 +566,11 @@
                     dh = dh + lax.dot_general(left, w1g[j * DQ:(j + 1) * DQ, :], NT, preferred_element_type=F32)
                 rs_put(STEPS + n, dh)
             rs_first(STEPS + n)
+
+        @pl.when((s >= DIRECT - 1) & (s < STEPS - 1))
+        def _():
+            with jax.named_scope("p3_cross"):
+                dy_cross(s + 1)
 
         @pl.when(s < STEPS)
         def _():
@@ -557,10 +599,6 @@
             swap(0, s, 1).start()
             swap(1, s, 1).start()
 
-            @pl.when(s < STEPS - 1)
-            def _():
-                with jax.named_scope("p3_nextl"):
-                    next_loads(s + 1)
         @pl.when(s == 0)
         def _():
             add_dw2(STEPS - 1)
@@ -583,20 +621,20 @@
         def _():
             w_load(s).start()
 
-        @pl.when(s < STEPS - DIRECT)
-        def _():
-            with jax.named_scope("p3_cross"):
-                dy_cross(s + DIRECT)
+        @pl.when(s < STEPS - 1)
+        def _():
+            with jax.named_scope("p3_nextl"):
+                next_loads(s + 1)
 
         @pl.when(s >= 4)
         def _():
             for k in TRIO:
                 st_copy(k, s - 4).start()
 
-        @pl.when(s >= 5)
+        @pl.when(s >= DX_LAG)
         def _():
             with jax.named_scope("p3_dx"):
-                dx_step(s - 5)
+                dx_step(s - DX_LAG)
         with jax.named_scope("p3_rsp"):
             rs_proc(K)
     loop(STEPS + 3, pass3)
@@ -610,8 +648,7 @@
         dg_copy(k).start()
 
     with jax.named_scope("t_dx"):
-        for s in (STEPS - 2, STEPS - 1):
-            dx_step(s)
+        loop(DX_LAG - 3, lambda s: dx_step(STEPS + 3 - DX_LAG + s))
     with jax.named_scope("t_dg"):
         for k in TRIO:
             dg_copy(k).wait_recv()
@@ -631,8 +668,10 @@
                 wait_bytes(xg.at[0], gs.at[arr, kind])
         for kind in (YA, ZA):
             wait_bytes(xown, gs.at[1, kind])
-        for kind in (X, YB, YBF, ZB):
+        for kind in (X, YB, ZB):
             wait_bytes(xown.at[0:DIRECT], gs.at[1, kind])
+        wait_bytes(xown.at[0:DIRECT - 1], gs.at[1, YBF])
+        wait_bytes(xown.at[0], gs.at[1, ZBF])
         wait_bytes(xown.at[0:N_YAF], gs.at[1, YAF])
         wait_bytes(xown.at[N_YAF:], gs.at[1, ZAF])
         wait_bytes(xg.at[0, DIRECT:], gs.at[1, XR])
@@ -691,10 +730,10 @@
                 pltpu.VMEM((3, 2, 2, ROWS, 256), F32), pltpu.VMEM((3, 2, ROWS, 256), F32),
                 pltpu.VMEM((8, DM), F32), pltpu.VMEM((8, DQ), F32),
                 pltpu.VMEM((STEPS, ROWS, 128), F32), pltpu.VMEM((TOK, 128), F32),
-                pltpu.VMEM((4, ROWS, DQ), F32),
+                pltpu.VMEM((DX_SLOTS, ROWS, DQ), F32),
                 pltpu.VMEM((STEPS, 8, 128), F32), pltpu.VMEM((3, STEPS, 8, 128), F32),
                 pltpu.VMEM((8, DQ), F32), pltpu.VMEM((3, 8, DQ), F32),
-                dma((2, 11)), dma((2, 6, STEPS)), dma((3, 3)), dma((3, 3)), d3, d3,
+                dma((2, 12)), dma((2, 6, STEPS)), dma((3, 3)), dma((3, 3)), d3, d3,
                 dma((2, 2, 2)), dma((2, 2, 2)), dma((4, 4)), dma((4, 4)),
                 d3, dma((3, STEPS)), d3, d3,
                 dma((8,)), dma((1,)), d2, d2, d2, d2, d2, d2,

time: 284 us -> 280 us (0.986)
  Pallas kernels: 283 us -> 279 us
    pallas_call x1, Pallas kernels: 277 us -> 274 us  [local_step(): pl.pallas_call(kernel, out_shape=[vm((STEPS, ROWS, DQ), BF16), vm((STEPS,...]
where the time goes in v4:
time: 280 us
  Pallas kernels  279 us (100%)
    pallas_call x1, Pallas kernels, local_step(): pl.pallas_call(kernel, out_shape=[vm((STEPS, ROWS, DQ), BF16), vm((STEPS,...  274 us
    pallas_call x1, Pallas kernels, local_step(): pl.pallas_call(finish, out_shape=[sd((STEPS, ROWS, DQ), BF16), sd((STEPS,...  5.85 us

profile of v4, /device:TPU:0, one launch (start us, length us, event | category | flops | bytes accessed | tf_op | source)
XLA Modules:
  0.0 280.3 jit_solution(3881597805812934002)
XLA Ops:
  0.6 273.6 %shard_map.109 = (bf16[8,128,512]{2,1,0:T(8,128)(2,1)S(1)}, bf16[8,128,512]{2,1,0:T(8,128)(2,1)S(1)}, f32[512,2048]{1,0:T(8,128)S(1)}, f32[512,2048]{1,0:T(8,128...) custom-call(bf16[8,128,512]{2,1,0:T(8,128)(2,1)} %bitcast.6, ...), custom_call_target="tpu_custom_call" | custom-call | tf_op jit(solution)/shard_map/pallas_call | solution.py:711
  274.3 5.9 %shard_map.110 = (bf16[8,128,512]{2,1,0:T(8,128)(2,1)}, bf16[8,128,512]{2,1,0:T(8,128)(2,1)}, f32[512,2048]{1,0:T(8,128)}, f32[512,2048]{1,0:T(8,128)}, f32[2048,512]{1,0:T(8,128)}, /*index=5*/f32[1,512]{1,0:T(1,128)}) custom-call(bf16[8,128,512]{2,1,0:T(8,128)(2,1)S(1)} %get-tuple-element.18.y_in, bf16[8,128,512]{2,1,0:T(8,128)(2,1)S(1)} %get-tuple-element.19.dx_in, ...), custom_call_target="tpu_custom_call" | custom-call | tf_op jit(solution)/shard_map/pallas_call | solution.py:746
